TPU v7x, 8 devices: a whole 2x2x1 slice. The times are simulated.
8 devices in a mesh: data: 8 (over z, y, x, core).
Axes of the slice: x: 2, y: 2, z: 1, core: 2. Of those that a mesh axis runs over, the one named last changes fastest.
Arguments:
- x_now: bfloat16 [32, 577, 1024], P('data')
- x_next: bfloat16 [32, 577, 1024], P('data')
- labels: int32 [32], P('data')
- w_up: float32 [6, 1024, 4096], replicated
- w_down: float32 [6, 4096, 1024], replicated
- w_head: float32 [1024, 1000], replicated
- mom_up: float32 [6, 1024, 4096], P(None, None, 'data')
- mom_down: float32 [6, 4096, 1024], P(None, 'data')
- mom_head: float32 [1024, 1000], P('data')
- learn_rate: float32 [], replicated
- mom_decay: float32 [], replicated
Outputs:
- output 1: float32 [32, 1000], P('data')
- output 2: float32 [6, 1024, 4096], replicated
- output 3: float32 [6, 4096, 1024], replicated
- output 4: float32 [1024, 1000], replicated
- output 5: float32 [6, 1024, 4096], P(None, None, 'data')
- output 6: float32 [6, 4096, 1024], P(None, 'data')
- output 7: float32 [1024, 1000], P('data')
All inputs are finite; a program needn't handle non-finite values.
Results may differ from a plain program's by a relative error of at most 0.011512.
Values are sent between devices in bfloat16 or wider.
A program may use at most 2 GiB of HBM per device.

v0:
```python
import jax
import jax.numpy as jnp
from jax import lax
from jax.sharding import PartitionSpec as P

LN_EPS = 1e-6
CONTRACT_ROWS = (((0,), (0,)), ((), ()))
CONTRACT_LAST = (((1,), (1,)), ((), ()))


def norm_rows(values):
    mean_v = jnp.mean(values, axis=-1, keepdims=True)
    centered = values - mean_v
    var_v = jnp.mean(centered * centered, axis=-1, keepdims=True)
    return centered * lax.rsqrt(var_v + LN_EPS)


def gelu_tanh(values):
    return jax.nn.gelu(values, approximate=True)


def block_forward(x_rows, up_w, down_w):
    x_wide = x_rows.astype(jnp.float32)
    u_rows = norm_rows(x_wide).astype(jnp.bfloat16)
    pre_act = jnp.dot(u_rows, up_w, preferred_element_type=jnp.float32).astype(jnp.bfloat16)
    gelu_out = gelu_tanh(pre_act.astype(jnp.float32)).astype(jnp.bfloat16)
    block_out = jnp.dot(gelu_out, down_w, preferred_element_type=jnp.float32).astype(jnp.bfloat16)
    new_rows = (x_wide + block_out.astype(jnp.float32)).astype(jnp.bfloat16)
    return new_rows, (x_rows, u_rows, pre_act, gelu_out)


def forward_rows(x_in, up_b, down_b):
    n_img, n_tok, width = x_in.shape
    rows = x_in.reshape(n_img * n_tok, width)
    saved_acts = []
    for layer in range(up_b.shape[0]):
        rows, layer_acts = block_forward(rows, up_b[layer], down_b[layer])
        saved_acts.append(layer_acts)
    return rows, saved_acts


def head_forward(rows, head_b, n_img):
    pooled = jnp.mean(rows.reshape(n_img, -1, rows.shape[-1]), axis=1, dtype=jnp.float32)
    normed = norm_rows(pooled).astype(jnp.bfloat16)
    return jnp.dot(normed, head_b, preferred_element_type=jnp.float32), pooled, normed


def backward_layers(saved_acts, up_b, down_b, grad_rows):
    up_grads = []
    down_grads = []
    for layer in reversed(range(len(saved_acts))):
        x_rows, u_rows, pre_act, gelu_out = saved_acts[layer]
        down_grads.append(lax.dot_general(gelu_out, grad_rows, CONTRACT_ROWS, preferred_element_type=jnp.float32).astype(jnp.bfloat16))
        grad_gelu = lax.dot_general(grad_rows, down_b[layer], CONTRACT_LAST, preferred_element_type=jnp.float32).astype(jnp.bfloat16)
        _, gelu_pull = jax.vjp(gelu_tanh, pre_act.astype(jnp.float32))
        grad_pre = gelu_pull(grad_gelu.astype(jnp.float32))[0].astype(jnp.bfloat16)
        up_grads.append(lax.dot_general(u_rows, grad_pre, CONTRACT_ROWS, preferred_element_type=jnp.float32).astype(jnp.bfloat16))
        if layer > 0:
            grad_u = lax.dot_general(grad_pre, up_b[layer], CONTRACT_LAST, preferred_element_type=jnp.float32).astype(jnp.bfloat16)
            _, norm_pull = jax.vjp(norm_rows, x_rows.astype(jnp.float32))
            grad_norm = norm_pull(grad_u.astype(jnp.float32))[0]
            grad_rows = (grad_rows.astype(jnp.float32) + grad_norm).astype(jnp.bfloat16)
    return jnp.stack(up_grads[::-1]), jnp.stack(down_grads[::-1])


def solution(mesh):
    n_dev = mesh.shape["data"]

    def local_step(x_now, x_next, labels, w_up, w_down, w_head, mom_up, mom_down, mom_head, learn_rate, mom_decay):
        n_img, n_tok, width = x_now.shape
        batch_total = n_img * n_dev
        up_b = w_up.astype(jnp.bfloat16)
        down_b = w_down.astype(jnp.bfloat16)
        head_b = w_head.astype(jnp.bfloat16)
        rows, saved_acts = forward_rows(x_now, up_b, down_b)
        logits, pooled, normed = head_forward(rows, head_b, n_img)
        soft_probs = jax.nn.softmax(logits, axis=-1)
        targets = jax.nn.one_hot(labels, logits.shape[-1], dtype=jnp.float32)
        grad_logits = ((soft_probs - targets) / batch_total).astype(jnp.bfloat16)
        head_grad = lax.dot_general(normed, grad_logits, CONTRACT_ROWS, preferred_element_type=jnp.float32).astype(jnp.bfloat16)
        grad_normed = lax.dot_general(grad_logits, head_b, CONTRACT_LAST, preferred_element_type=jnp.float32).astype(jnp.bfloat16)
        _, norm_pull = jax.vjp(norm_rows, pooled)
        grad_pooled = norm_pull(grad_normed.astype(jnp.float32))[0]
        grad_rows = jnp.broadcast_to((grad_pooled / n_tok)[:, None, :], (n_img, n_tok, width))
        grad_rows = grad_rows.astype(jnp.bfloat16).reshape(n_img * n_tok, width)
        up_grad, down_grad = backward_layers(saved_acts, up_b, down_b, grad_rows)
        up_sum = lax.psum_scatter(up_grad, "data", scatter_dimension=2, tiled=True)
        down_sum = lax.psum_scatter(down_grad, "data", scatter_dimension=1, tiled=True)
        head_sum = lax.psum_scatter(head_grad, "data", scatter_dimension=0, tiled=True)
        shard_index = lax.axis_index("data")
        new_mom_up = mom_decay * mom_up + up_sum.astype(jnp.float32)
        new_mom_down = mom_decay * mom_down + down_sum.astype(jnp.float32)
        new_mom_head = mom_decay * mom_head + head_sum.astype(jnp.float32)
        up_width = mom_up.shape[2]
        down_width = mom_down.shape[1]
        head_width = mom_head.shape[0]
        up_part = lax.dynamic_slice_in_dim(w_up, shard_index * up_width, up_width, axis=2) - learn_rate * new_mom_up
        down_part = lax.dynamic_slice_in_dim(w_down, shard_index * down_width, down_width, axis=1) - learn_rate * new_mom_down
        head_part = lax.dynamic_slice_in_dim(w_head, shard_index * head_width, head_width, axis=0) - learn_rate * new_mom_head
        new_w_up = lax.all_gather(up_part, "data", axis=2, tiled=True)
        new_w_down = lax.all_gather(down_part, "data", axis=1, tiled=True)
        new_w_head = lax.all_gather(head_part, "data", axis=0, tiled=True)
        next_rows, _ = forward_rows(x_next, new_w_up.astype(jnp.bfloat16), new_w_down.astype(jnp.bfloat16))
        logits_next = head_forward(next_rows, new_w_head.astype(jnp.bfloat16), n_img)[0]
        return (logits_next, new_w_up, new_w_down, new_w_head, new_mom_up, new_mom_down, new_mom_head)

    spec_up = P(None, None, "data")
    spec_down = P(None, "data", None)
    spec_head = P("data", None)
    return jax.shard_map(
        local_step,
        mesh=mesh,
        in_specs=(P("data"), P("data"), P("data"), P(), P(), P(), spec_up, spec_down, spec_head, P(), P()),
        out_specs=(P("data"), P(), P(), P(), spec_up, spec_down, spec_head),
        check_vma=False,
    )
```

profile of v0, /device:TPU:0, one launch (start us, length us, event | category | flops | bytes accessed | tf_op | source)
XLA Modules:
  0.0 3257.1 jit_solution(14134050045892899680)
XLA Ops:
  19.3 48.1 %convert_element_type.549 = bf16[6,1024,4096]{2,1,0:T(8,128)(2,1)} convert(f32[6,1024,4096]{2,1,0:T(8,128)} %param.14) | non-fusion elementwise | flops 25165824 | bytes 150994944 | tf_op jit(solution)/shard_map/convert_element_type | solution.py:72
  88.8 48.0 %convert_element_type.553 = bf16[6,4096,1024]{2,1,0:T(8,128)(2,1)} convert(f32[6,4096,1024]{2,1,0:T(8,128)} %param.15) | non-fusion elementwise | flops 25165824 | bytes 150994944 | tf_op jit(solution)/shard_map/convert_element_type | solution.py:73
  172.3 32.5 convert_reduce_fusion.9
  234.0 33.9 %convert_reduce_fusion.8 = (f32[2308]{0:T(1024)S(1)}, bf16[2308,1024]{1,0:T(8,128)(2,1)S(1)}) fusion(bf16[6,4096,1024]{2,1,0:T(8,128)(2,1)} %convert_element_type.553, bf16[2308,4096]{1,0:T(8,128)(2,1)} %convolution_convert_fusion.16, bf16[2308,1024]{1,0:T(8,128)(2,1)S(1)} %get-tuple-element.16), kind=kOutput, calls=%fused_computation.223 | convolution fusion | flops 19471984640 | bytes 36791312 | tf_op jit(solution)/shard_map/dot_general | solution.py:27
  299.7 33.8 %convert_reduce_fusion.7 = (f32[2308]{0:T(1024)S(1)}, bf16[2308,1024]{1,0:T(8,128)(2,1)S(1)}) fusion(bf16[6,4096,1024]{2,1,0:T(8,128)(2,1)} %convert_element_type.553, bf16[2308,4096]{1,0:T(8,128)(2,1)} %convolution_convert_fusion.15, bf16[2308,1024]{1,0:T(8,128)(2,1)S(1)} %copy-done.3), kind=kOutput, calls=%fused_computation.216 | convolution fusion | flops 19471984640 | bytes 36791312 | tf_op jit(solution)/shard_map/dot_general | solution.py:27
  365.6 33.9 %convert_reduce_fusion.6 = (f32[2308]{0:T(1024)S(1)}, bf16[2308,1024]{1,0:T(8,128)(2,1)S(1)}) fusion(bf16[6,4096,1024]{2,1,0:T(8,128)(2,1)} %convert_element_type.553, bf16[2308,4096]{1,0:T(8,128)(2,1)} %convolution_convert_fusion.14, bf16[2308,1024]{1,0:T(8,128)(2,1)S(1)} %copy-done.5), kind=kOutput, calls=%fused_computation.209 | convolution fusion | flops 19471984640 | bytes 36791312 | tf_op jit(solution)/shard_map/dot_general | solution.py:27
  431.3 33.8 %convert_reduce_fusion.5 = (f32[2308]{0:T(1024)S(1)}, bf16[2308,1024]{1,0:T(8,128)(2,1)S(1)}) fusion(bf16[6,4096,1024]{2,1,0:T(8,128)(2,1)} %convert_element_type.553, bf16[2308,4096]{1,0:T(8,128)(2,1)} %convolution_convert_fusion.13, bf16[2308,1024]{1,0:T(8,128)(2,1)S(1)} %copy-done.7), kind=kOutput, calls=%fused_computation.202 | convolution fusion | flops 19471984640 | bytes 36791312 | tf_op jit(solution)/shard_map/dot_general | solution.py:27
  561.0 49.6 %fusion.8 = bf16[2308,4096]{1,0:T(8,128)(2,1)} fusion(bf16[2308,4096]{1,0:T(8,128)(2,1)} %convolution_convert_fusion.12, bf16[2308,1024]{1,0:T(8,128)(2,1)} %reshape.326, bf16[6,4096,1024]{2,1,0:T(8,128)(2,1)} %convert_element_type.553), kind=kOutput, calls=%fused_computation.68 | convolution fusion | flops 19578339328 | bytes 50970624 | tf_op jit(solution)/shard_map/dot_general | solution.py:54
  650.0 49.7 %fusion.11 = bf16[2308,4096]{1,0:T(8,128)(2,1)} fusion(bf16[2308,4096]{1,0:T(8,128)(2,1)} %convolution_convert_fusion.13, bf16[2308,1024]{1,0:T(8,128)(2,1)} %add_convert_fusion.5, bf16[6,4096,1024]{2,1,0:T(8,128)(2,1)} %convert_element_type.553), kind=kOutput, calls=%fused_computation.71 | convolution fusion | flops 19578339328 | bytes 50970624 | tf_op jit(solution)/shard_map/dot_general | solution.py:54
  738.9 50.0 %fusion.14 = bf16[2308,4096]{1,0:T(8,128)(2,1)} fusion(bf16[2308,4096]{1,0:T(8,128)(2,1)} %convolution_convert_fusion.14, bf16[2308,1024]{1,0:T(8,128)(2,1)} %add_convert_fusion.4, bf16[6,4096,1024]{2,1,0:T(8,128)(2,1)} %convert_element_type.553), kind=kOutput, calls=%fused_computation.74 | convolution fusion | flops 19578339328 | bytes 50970624 | tf_op jit(solution)/shard_map/dot_general | solution.py:54
  828.0 49.8 %fusion.17 = bf16[2308,4096]{1,0:T(8,128)(2,1)} fusion(bf16[2308,4096]{1,0:T(8,128)(2,1)} %convolution_convert_fusion.15, bf16[2308,1024]{1,0:T(8,128)(2,1)} %add_convert_fusion.3, bf16[6,4096,1024]{2,1,0:T(8,128)(2,1)} %convert_element_type.553), kind=kOutput, calls=%fused_computation.77 | convolution fusion | flops 19578339328 | bytes 50970624 | tf_op jit(solution)/shard_map/dot_general | solution.py:54
  913.7 49.8 %fusion.20 = bf16[2308,4096]{1,0:T(8,128)(2,1)} fusion(bf16[2308,4096]{1,0:T(8,128)(2,1)} %convolution_convert_fusion.16, bf16[2308,1024]{1,0:T(8,128)(2,1)} %add_convert_fusion.2, bf16[6,4096,1024]{2,1,0:T(8,128)(2,1)} %convert_element_type.553), kind=kOutput, calls=%fused_computation.80 | convolution fusion | flops 19578339328 | bytes 50970624 | tf_op jit(solution)/shard_map/dot_general | solution.py:54
  994.2 52.8 %fusion.23.clone.5 = bf16[2308,4096]{1,0:T(8,128)(2,1)} fusion(bf16[2308,4096]{1,0:T(8,128)(2,1)} %convolution_convert_fusion.17, bf16[6,4096,1024]{2,1,0:T(8,128)(2,1)} %convert_element_type.553, bf16[2308,1024]{1,0:T(8,128)(2,1)} %add_convert_fusion.2, bf16[2308,1024]{1,0:T(8,128)(2,1)} %copy-done, bf16[2308,1024]{1,0:T(8,128)(2,1)} %copy-done.10, ...), kind=kOutput, calls=%fused_computation.83.clone.clone.clone.2 | convolution fusion | flops 19604336640 | bytes 60477504 | tf_op jit(solution)/shard_map/dot_general | solution.py:54
  1233.2 33.1 %bitcast_dynamic-update-slice_fusion.5 = bf16[6,4096,1024]{2,1,0:T(8,128)(2,1)} fusion(bf16[2308,4096]{1,0:T(8,128)(2,1)} %convolution_convert_fusion.17, bf16[2308,1024]{1,0:T(8,128)(2,1)S(1)} %add_convert_fusion.16), kind=kOutput, calls=%fused_computation.336 | convolution fusion | flops 19459637248 | bytes 32022528 | tf_op jit(solution)/shard_map/dot_general | solution.py:53
  1266.3 33.4 %bitcast_dynamic-update-slice_fusion.4 = bf16[6,4096,1024]{2,1,0:T(8,128)(2,1)} fusion(bf16[6,4096,1024]{2,1,0:T(8,128)(2,1)} %bitcast_dynamic-update-slice_fusion.5, bf16[2308,1024]{1,0:T(8,128)(2,1)S(1)} %bitcast.361, bf16[2308,4096]{1,0:T(8,128)(2,1)} %convolution_convert_fusion.16), kind=kOutput, calls=%fused_computation.335 | convolution fusion | flops 19459637248 | bytes 32055296 | tf_op jit(solution)/shard_map/dot_general | solution.py:53
  1299.7 33.4 %bitcast_dynamic-update-slice_fusion.3 = bf16[6,4096,1024]{2,1,0:T(8,128)(2,1)} fusion(bf16[6,4096,1024]{2,1,0:T(8,128)(2,1)} %bitcast_dynamic-update-slice_fusion.4, bf16[2308,1024]{1,0:T(8,128)(2,1)S(1)} %bitcast.359, bf16[2308,4096]{1,0:T(8,128)(2,1)} %convolution_convert_fusion.15), kind=kOutput, calls=%fused_computation.334 | convolution fusion | flops 19459637248 | bytes 32055296 | tf_op jit(solution)/shard_map/dot_general | solution.py:53
  1333.2 33.5 %bitcast_dynamic-update-slice_fusion.2 = bf16[6,4096,1024]{2,1,0:T(8,128)(2,1)} fusion(bf16[6,4096,1024]{2,1,0:T(8,128)(2,1)} %bitcast_dynamic-update-slice_fusion.3, bf16[2308,1024]{1,0:T(8,128)(2,1)S(1)} %bitcast.355, bf16[2308,4096]{1,0:T(8,128)(2,1)} %convolution_convert_fusion.14), kind=kOutput, calls=%fused_computation.333 | convolution fusion | flops 19459637248 | bytes 32055296 | tf_op jit(solution)/shard_map/dot_general | solution.py:53
  1366.7 33.8 %bitcast_dynamic-update-slice_fusion.1 = bf16[6,4096,1024]{2,1,0:T(8,128)(2,1)} fusion(bf16[6,4096,1024]{2,1,0:T(8,128)(2,1)} %bitcast_dynamic-update-slice_fusion.2, bf16[2308,1024]{1,0:T(8,128)(2,1)S(1)} %bitcast.351, bf16[2308,4096]{1,0:T(8,128)(2,1)} %convolution_convert_fusion.13), kind=kOutput, calls=%fused_computation.332 | convolution fusion | flops 19459637248 | bytes 32055296 | tf_op jit(solution)/shard_map/dot_general | solution.py:53
  1436.4 65.3 %reduce-scatter.6.cloned.1.call-done = bf16[6,1024,512]{2,1,0:T(8,128)(2,1)} async-done(((bf16[6,1024,4096]{2,1,0:T(8,128)(2,1)}), bf16[6,1024,512]{2,1,0:T(8,128)(2,1)}) %reduce-scatter.6.cloned.1.call-update) | async-done | bytes 6291472 | tf_op jit(solution)/shard_map/reduce_scatter | solution.py:87
  1522.6 257.7 %reduce-scatter.8.cloned.1.call-done = bf16[6,512,1024]{2,1,0:T(8,128)(2,1)} async-done(((bf16[6,4096,1024]{2,1,0:T(8,128)(2,1)}), bf16[6,512,1024]{2,1,0:T(8,128)(2,1)}) %reduce-scatter.8.cloned.1.call-update) | async-done | bytes 6291472 | tf_op jit(solution)/shard_map/reduce_scatter | solution.py:88
  1836.7 418.5 %all-gather.4.cloned.1.call-done = f32[6,1024,4096]{2,1,0:T(8,128)} async-done(((f32[6,1024,512]{2,1,0:T(8,128)}), f32[6,1024,4096]{2,1,0:T(8,128)}) %all-gather.4.cloned.1.call-update) | async-done | bytes 100663312 | tf_op jit(solution)/shard_map/all_gather | solution.py:100
  2255.2 48.0 %convert_element_type.651 = bf16[6,1024,4096]{2,1,0:T(8,128)(2,1)} convert(f32[6,1024,4096]{2,1,0:T(8,128)} %all-gather.4.cloned.1.call-done) | non-fusion elementwise | flops 25165824 | bytes 150994944 | tf_op jit(solution)/shard_map/convert_element_type | solution.py:103
  2303.1 33.0 %fusion.35.clone.5.clone.5 = bf16[2308,4096]{1,0:T(8,128)(2,1)} fusion(bf16[2308,1024]{1,0:T(8,128)(2,1)} %convert_element_type.542, bf16[6,1024,4096]{2,1,0:T(8,128)(2,1)} %convert_element_type.651), kind=kOutput, calls=%fused_computation.95.clone.clone.clone.clone.clone.clone.clone.clone.clone.2 | convolution fusion | flops 19464896512 | bytes 32030720 | tf_op jit(solution)/shard_map/dot_general | solution.py:25
  2336.1 360.6 %all-gather.6.cloned.1.call-done = f32[6,4096,1024]{2,1,0:T(8,128)} async-done(((f32[6,512,1024]{2,1,0:T(8,128)}), f32[6,4096,1024]{2,1,0:T(8,128)}) %all-gather.6.cloned.1.call-update) | async-done | bytes 100663312 | tf_op jit(solution)/shard_map/all_gather | solution.py:101
  2696.7 48.0 %convert_element_type.662 = bf16[6,4096,1024]{2,1,0:T(8,128)(2,1)} convert(f32[6,4096,1024]{2,1,0:T(8,128)} %all-gather.6.cloned.1.call-done) | non-fusion elementwise | flops 25165824 | bytes 150994944 | tf_op jit(solution)/shard_map/convert_element_type | solution.py:103
  2774.6 32.2 fusion.41.clone.5.clone.5
  2838.7 33.8 %fusion.47.clone.5.clone.5 = bf16[2308,4096]{1,0:T(8,128)(2,1)} fusion(bf16[6,1024,4096]{2,1,0:T(8,128)(2,1)} %convert_element_type.651, bf16[2308,1024]{1,0:T(8,128)(2,1)} %copy-done.16, f32[2308]{0:T(1024)S(1)} %add_rsqrt_fusion.5, f32[2308]{0:T(1024)S(1)} %broadcast_multiply_fusion.5), kind=kOutput, calls=%fused_computation.107.clone.clone.clone.clone.clone.clone.clone.clone.clone.2 | convolution fusion | flops 19474350080 | bytes 32049184 | tf_op jit(solution)/shard_map/dot_general | solution.py:25
  2904.6 33.8 %fusion.53.clone.5.clone.5 = bf16[2308,4096]{1,0:T(8,128)(2,1)} fusion(bf16[6,1024,4096]{2,1,0:T(8,128)(2,1)} %convert_element_type.651, bf16[2308,1024]{1,0:T(8,128)(2,1)} %copy-done.18, f32[2308]{0:T(1024)S(1)} %add_rsqrt_fusion.4, f32[2308]{0:T(1024)S(1)} %broadcast_multiply_fusion.4), kind=kOutput, calls=%fused_computation.113.clone.clone.clone.clone.clone.clone.clone.clone.clone.2 | convolution fusion | flops 19474350080 | bytes 32049184 | tf_op jit(solution)/shard_map/dot_general | solution.py:25
  2970.2 33.8 %fusion.59.clone.5.clone.5 = bf16[2308,4096]{1,0:T(8,128)(2,1)} fusion(bf16[6,1024,4096]{2,1,0:T(8,128)(2,1)} %convert_element_type.651, bf16[2308,1024]{1,0:T(8,128)(2,1)} %copy-done.20, f32[2308]{0:T(1024)S(1)} %add_rsqrt_fusion.3, f32[2308]{0:T(1024)S(1)} %broadcast_multiply_fusion.3), kind=kOutput, calls=%fused_computation.119.clone.clone.clone.clone.clone.clone.clone.clone.clone.2 | convolution fusion | flops 19474350080 | bytes 32049184 | tf_op jit(solution)/shard_map/dot_general | solution.py:25
  3035.9 33.8 %fusion.65.clone.9 = bf16[2308,4096]{1,0:T(8,128)(2,1)} fusion(bf16[6,1024,4096]{2,1,0:T(8,128)(2,1)} %convert_element_type.651, bf16[2308,1024]{1,0:T(8,128)(2,1)} %copy-done.22, f32[2308]{0:T(1024)S(1)} %add_rsqrt_fusion.2, f32[2308]{0:T(1024)S(1)} %broadcast_multiply_fusion.2), kind=kOutput, calls=%fused_computation.125.clone.clone.clone.clone.clone.clone.clone.2 | convolution fusion | flops 19474350080 | bytes 32049184 | tf_op jit(solution)/shard_map/dot_general | solution.py:25
  3113.3 66.2 %copy.67 = f32[6,1024,4096]{2,1,0:T(8,128)} copy(f32[6,1024,4096]{2,1,0:T(8,128)} %all-gather.4.cloned.1.call-done) | data formatting | bytes 201326592
  3179.4 65.8 %copy.68 = f32[6,4096,1024]{2,1,0:T(8,128)} copy(f32[6,4096,1024]{2,1,0:T(8,128)} %all-gather.6.cloned.1.call-done) | data formatting | bytes 201326592
  (388 shorter events, 976.6 us)
Async XLA Ops:
  7.2 1425.8 %reduce-scatter.10.cloned.1.call-start = ((), (), s32[]{:S(2)}) async-start(), calls=%async_computation.8 | async-start | bytes 2359296
  465.1 176.5 %copy-start.38 = (f32[2308]{0:T(1024)}, f32[2308]{0:T(1024)S(1)}, u32[]{:S(2)}) copy-start(f32[2308]{0:T(1024)S(1)} %broadcast_multiply_fusion.7) | copy-start | bytes 27700
  547.8 953.8 %reduce-scatter.6.cloned.1.call-start = ((), (), s32[]{:S(2)}) async-start(), calls=%async_computation.3 | async-start | bytes 56623104 | tf_op jit(solution)/shard_map/reduce_scatter | solution.py:87
  555.2 55.5 %slice-start.16 = ((s8[4734976]{0:T(1024)(128)(4,1)}), s8[540672]{0:T(1024)(128)(4,1)S(1)}, s32[]{:S(2)}) async-start(s8[4734976]{0:T(1024)(128)(4,1)} %bitcast.340), calls=%async_computation.25 | async-start | bytes 1081344
  642.8 57.0 %slice-start.12 = ((s8[4734976]{0:T(1024)(128)(4,1)}), s8[4194304]{0:T(1024)(128)(4,1)S(1)}, s32[]{:S(2)}) async-start(s8[4734976]{0:T(1024)(128)(4,1)} %bitcast.336), calls=%async_computation.21 | async-start | bytes 8388608
  731.6 57.3 %slice-start.8 = ((s8[4734976]{0:T(1024)(128)(4,1)}), s8[4194304]{0:T(1024)(128)(4,1)S(1)}, s32[]{:S(2)}) async-start(s8[4734976]{0:T(1024)(128)(4,1)} %bitcast.332), calls=%async_computation.17 | async-start | bytes 8388608
  738.9 50.0 %slice-start.9 = ((s8[4734976]{0:T(1024)(128)(4,1)}), s8[540672]{0:T(1024)(128)(4,1)S(1)}, s32[]{:S(2)}) async-start(s8[4734976]{0:T(1024)(128)(4,1)} %bitcast.332), calls=%async_computation.18 | async-start | bytes 1081344
  738.9 50.0 %copy-start.33 = (f32[2308]{0:T(1024)S(1)}, f32[2308]{0:T(1024)}, u32[]{:S(2)}) copy-start(f32[2308]{0:T(1024)} %copy-done.32) | copy-start | bytes 27700
  820.7 57.0 %slice-start.4 = ((s8[4734976]{0:T(1024)(128)(4,1)}), s8[4194304]{0:T(1024)(128)(4,1)S(1)}, s32[]{:S(2)}) async-start(s8[4734976]{0:T(1024)(128)(4,1)} %bitcast.328), calls=%async_computation.13 | async-start | bytes 8388608
  908.6 54.9 %slice-start.2 = ((s8[4734976]{0:T(1024)(128)(4,1)}), s8[4194304]{0:T(1024)(128)(4,1)S(1)}, s32[]{:S(2)}) async-start(s8[4734976]{0:T(1024)(128)(4,1)} %bitcast.326), calls=%async_computation.11 | async-start | bytes 8388608
  913.7 49.8 %slice-start.3 = ((s8[4734976]{0:T(1024)(128)(4,1)}), s8[540672]{0:T(1024)(128)(4,1)S(1)}, s32[]{:S(2)}) async-start(s8[4734976]{0:T(1024)(128)(4,1)} %bitcast.326), calls=%async_computation.12 | async-start | bytes 1081344
  913.7 49.8 %copy-start.28 = (f32[2308]{0:T(1024)S(1)}, f32[2308]{0:T(1024)}, u32[]{:S(2)}) copy-start(f32[2308]{0:T(1024)} %copy-done.27) | copy-start | bytes 27700
  991.4 55.5 %copy-start.54 = (f32[2308]{0:T(1024)}, f32[2308]{0:T(1024)S(1)}, u32[]{:S(2)}) copy-start(f32[2308]{0:T(1024)S(1)} %multiply_multiply_fusion) | copy-start | bytes 27700
  994.1 52.8 %copy-start.66 = (f32[2308]{0:T(1024)}, f32[2308]{0:T(1024)S(1)}, u32[]{:S(2)}) copy-start(f32[2308]{0:T(1024)S(1)} %negate_multiply_fusion) | copy-start | bytes 27700
  994.2 52.8 %copy-start.68 = (f32[4,577]{1,0:T(4,128)S(1)}, f32[4,577]{1,0:T(4,128)}, u32[]{:S(2)}) copy-start(f32[4,577]{1,0:T(4,128)} %copy.51) | copy-start | bytes 27700
  994.2 52.9 %copy-start.69 = (f32[4,577]{1,0:T(4,128)S(1)}, f32[4,577]{1,0:T(4,128)}, u32[]{:S(2)}) copy-start(f32[4,577]{1,0:T(4,128)} %copy.50) | copy-start | bytes 27700
  1047.1 60.8 %slice-start.6 = ((s8[4734976]{0:T(1024)(128)(4,1)}), s8[4194304]{0:T(1024)(128)(4,1)S(1)}, s32[]{:S(2)}) async-start(s8[4734976]{0:T(1024)(128)(4,1)} %bitcast.330), calls=%async_computation.15 | async-start | bytes 8388608
  1078.8 58.4 %slice-start.10 = ((s8[4734976]{0:T(1024)(128)(4,1)}), s8[4194304]{0:T(1024)(128)(4,1)S(1)}, s32[]{:S(2)}) async-start(s8[4734976]{0:T(1024)(128)(4,1)} %bitcast.334), calls=%async_computation.19 | async-start | bytes 8388608
  1107.9 58.2 %slice-start.14 = ((s8[4734976]{0:T(1024)(128)(4,1)}), s8[4194304]{0:T(1024)(128)(4,1)S(1)}, s32[]{:S(2)}) async-start(s8[4734976]{0:T(1024)(128)(4,1)} %bitcast.338), calls=%async_computation.23 | async-start | bytes 8388608
  1137.3 58.1 %slice-start.18 = ((s8[4734976]{0:T(1024)(128)(4,1)}), s8[4194304]{0:T(1024)(128)(4,1)S(1)}, s32[]{:S(2)}) async-start(s8[4734976]{0:T(1024)(128)(4,1)} %bitcast.342), calls=%async_computation.27 | async-start | bytes 8388608
  1224.1 556.2 %reduce-scatter.8.cloned.1.call-start = ((), (), s32[]{:S(2)}) async-start(), calls=%async_computation.5 | async-start | bytes 56623104 | tf_op jit(solution)/shard_map/reduce_scatter | solution.py:88
  1224.8 74.9 %slice-start.34 = ((s8[4734976]{0:T(1024)(128)(4,1)}), s8[4194304]{0:T(1024)(128)(4,1)S(1)}, s32[]{:S(2)}) async-start(s8[4734976]{0:T(1024)(128)(4,1)} %bitcast.358), calls=%async_computation.43 | async-start | bytes 8388608
  1233.2 66.5 %slice-start.35 = ((s8[4734976]{0:T(1024)(128)(4,1)}), s8[540672]{0:T(1024)(128)(4,1)S(1)}, s32[]{:S(2)}) async-start(s8[4734976]{0:T(1024)(128)(4,1)} %bitcast.358), calls=%async_computation.44 | async-start | bytes 1081344
  1266.3 66.8 %slice-start.30 = ((s8[4734976]{0:T(1024)(128)(4,1)}), s8[4194304]{0:T(1024)(128)(4,1)S(1)}, s32[]{:S(2)}) async-start(s8[4734976]{0:T(1024)(128)(4,1)} %bitcast.354), calls=%async_computation.39 | async-start | bytes 8388608
  1299.7 66.9 %slice-start.26 = ((s8[4734976]{0:T(1024)(128)(4,1)}), s8[4194304]{0:T(1024)(128)(4,1)S(1)}, s32[]{:S(2)}) async-start(s8[4734976]{0:T(1024)(128)(4,1)} %bitcast.350), calls=%async_computation.35 | async-start | bytes 8388608
  1333.1 67.3 %slice-start.22 = ((s8[4734976]{0:T(1024)(128)(4,1)}), s8[4194304]{0:T(1024)(128)(4,1)S(1)}, s32[]{:S(2)}) async-start(s8[4734976]{0:T(1024)(128)(4,1)} %bitcast.346), calls=%async_computation.31 | async-start | bytes 8388608
  1333.1 67.3 %slice-start.38 = ((s8[18939904]{0:T(1024)(128)(4,1)}), s8[2162688]{0:T(1024)(128)(4,1)S(1)}, s32[]{:S(2)}) async-start(s8[18939904]{0:T(1024)(128)(4,1)} %bitcast.362), calls=%async_computation.47 | async-start | bytes 4325376
  1333.2 67.3 %slice-start.39 = ((s8[18939904]{0:T(1024)(128)(4,1)}), s8[4194304]{0:T(1024)(128)(4,1)S(1)}, s32[]{:S(2)}) async-start(s8[18939904]{0:T(1024)(128)(4,1)} %bitcast.362), calls=%async_computation.48 | async-start | bytes 8388608
  1333.2 67.3 %slice-start.40 = ((s8[18939904]{0:T(1024)(128)(4,1)}), s8[4194304]{0:T(1024)(128)(4,1)S(1)}, s32[]{:S(2)}) async-start(s8[18939904]{0:T(1024)(128)(4,1)} %bitcast.362), calls=%async_computation.49 | async-start | bytes 8388608
  1431.6 405.1 %all-gather.8.cloned.1.call-start = ((), (), s32[]{:S(2)}) async-start(), calls=%async_computation.7 | async-start | bytes 4608000 | tf_op jit(solution)/shard_map/all_gather | solution.py:102
  1436.3 818.9 %all-gather.4.cloned.1.call-start = ((), (), s32[]{:S(2)}) async-start(), calls=%async_computation.4 | async-start | bytes 113246208 | tf_op jit(solution)/shard_map/all_gather | solution.py:100
  1522.5 1174.2 %all-gather.6.cloned.1.call-start = ((), (), s32[]{:S(2)}) async-start(), calls=%async_computation.6 | async-start | bytes 113246208 | tf_op jit(solution)/shard_map/all_gather | solution.py:101
  (88 other events, 1850.0 us)
Sparse Core Ops, SparseCore 0:
  547.9 35.4 reduce-scatter.9
  1224.2 277.3 reduce-scatter.5
  1505.8 274.5 reduce-scatter.7
  1782.5 31.0 all-gather.7
  1815.9 439.1 all-gather.3
  2257.5 439.1 all-gather.5
where the time goes:
time: 3260 us
  matrix products  1560 us (48%)
  waiting for transfers between devices  1100 us (34%)
  other arithmetic  334 us (10%)
  local copies, waits for them, and re-layouts  244 us (7%)
    all_gather x1, waiting for transfers between devices, local_step(): new_w_up = lax.all_gather(up_part, 'data', axis=2, tiled=True)  419 us
    dot_general x12, matrix products, block_forward(): jnp.dot(gelu_out, down_w, preferred_element_type=jnp.float32)  368 us
    dot_general x12, matrix products, block_forward(): jnp.dot(u_rows, up_w, preferred_element_type=jnp.float32)  365 us
    all_gather x1, waiting for transfers between devices, local_step(): new_w_down = lax.all_gather(down_part, 'data', axis=1, tiled=True)  361 us
    dot_general x6, matrix products, backward_layers(): lax.dot_general(grad_rows, down_b[layer], CONTRACT_LAST, preferred_elemen...  302 us
    reduce_scatter x1, waiting for transfers between devices, local_step(): lax.psum_scatter(down_grad, 'data', scatter_dimension=1, tiled=True)  258 us
    dot_general x6, matrix products, backward_layers(): lax.dot_general(gelu_out, grad_rows, CONTRACT_ROWS, preferred_element_typ...  198 us
    dot_general x6, matrix products, backward_layers(): lax.dot_general(u_rows, grad_pre, CONTRACT_ROWS, preferred_element_type=j...  177 us
  transfers between devices with their start and end apart: 6, of which 4 were waited for; matrix products, arithmetic and copies ran while one was open for 32% of the time, Pallas kernels for 0%

commit v1 on v0

v1 whole, which is shorter than its diff:
```python
import functools

import jax
import jax.numpy as jnp
from jax import lax
from jax.experimental import pallas as pl
from jax.experimental.pallas import tpu as pltpu
from jax.sharding import PartitionSpec as P


LN_EPS = 1e-6
GELU_A = 0.7978845608028654
GELU_B = GELU_A * 0.044715
BF = jnp.bfloat16
F32 = jnp.float32
CONTRACT_ROWS = (((0,), (0,)), ((), ()))
CONTRACT_LAST = (((1,), (1,)), ((), ()))
ONCE = pl.Buffered(1)
ROW_BLOCKS = 5
EARLY = 3


def norm_rows(values):
    mean_v = jnp.mean(values, axis=-1, keepdims=True)
    centered = values - mean_v
    var_v = jnp.mean(centered * centered, axis=-1, keepdims=True)
    return centered * lax.rsqrt(var_v + LN_EPS)


def gelu_tanh(a):
    t = jnp.tanh(a * (GELU_A + GELU_B * (a * a)))
    return a * (0.5 + 0.5 * t)


def row_slice(r, size):
    return pl.ds(pl.multiple_of(r * size, 16), size)


def fwd_now_body(x_ref, wu_ref, wd_ref, a_ref, xo_ref, x_s, u_s, acc_s):
    layer, c = pl.program_id(0), pl.program_id(1)
    last = pl.num_programs(1) - 1
    rb = x_s.shape[0] // ROW_BLOCKS

    @pl.when((layer == 0) & (c == 0))
    def _():
        @pl.loop(0, ROW_BLOCKS)
        def _(r):
            rs = row_slice(r, rb)
            x = x_ref[rs, :]
            x_s[rs, :] = x
            u_s[rs, :] = norm_rows(x.astype(F32)).astype(BF)
            acc_s[rs, :] = jnp.zeros((rb, x.shape[1]), F32)

    wu = wu_ref[...].astype(BF)
    wd = wd_ref[...].astype(BF)

    def up(r):
        rs = pl.ds(r * rb, rb)
        a = jnp.dot(u_s[rs, :], wu, preferred_element_type=F32).astype(BF)
        a_ref[rs, :] = a
        return gelu_tanh(a.astype(F32)).astype(BF)

    z = up(0)
    for r in range(ROW_BLOCKS):
        z_next = up(r + 1) if r + 1 < ROW_BLOCKS else None
        acc_s[pl.ds(r * rb, rb), :] += jnp.dot(z, wd, preferred_element_type=F32)
        z = z_next

    @pl.when(c == last)
    def _():
        @pl.loop(0, ROW_BLOCKS)
        def _(r):
            rs = row_slice(r, rb)
            x = (x_s[rs, :].astype(F32) + acc_s[rs, :].astype(BF).astype(F32)).astype(BF)
            x_s[rs, :] = x
            xo_ref[rs, :] = x
            u_s[rs, :] = norm_rows(x.astype(F32)).astype(BF)
            acc_s[rs, :] = jnp.zeros((rb, x.shape[1]), F32)


def fwd_now(x, w_up, w_down, n_chunk):
    rows, width = x.shape
    layers, _, hidden = w_up.shape
    ch = hidden // n_chunk
    return pl.pallas_call(
        fwd_now_body,
        grid=(layers, n_chunk),
        in_specs=[
            pl.BlockSpec((rows, width), lambda l, c: (0, 0), pipeline_mode=ONCE),
            pl.BlockSpec((None, width, ch), lambda l, c: (l, 0, c)),
            pl.BlockSpec((None, ch, width), lambda l, c: (l, c, 0)),
        ],
        out_specs=[
            pl.BlockSpec((None, rows, ch), lambda l, c: (l, 0, c)),
            pl.BlockSpec((None, rows, width), lambda l, c: (l, 0, 0)),
        ],
        out_shape=[
            jax.ShapeDtypeStruct((layers, rows, hidden), BF),
            jax.ShapeDtypeStruct((layers, rows, width), BF),
        ],
        scratch_shapes=[
            pltpu.VMEM((rows, width), BF),
            pltpu.VMEM((rows, width), BF),
            pltpu.VMEM((rows, width), F32),
        ],
        compiler_params=pltpu.CompilerParams(
            vmem_limit_bytes=62 * 2**20, dimension_semantics=("arbitrary", "arbitrary")
        ),
        cost_estimate=pl.CostEstimate(
            flops=layers * 4 * rows * width * hidden,
            bytes_accessed=layers * (8 * width * hidden + 2 * rows * (width + hidden)),
            transcendentals=layers * rows * hidden,
        ),
        name="fwd_now",
    )(x, w_up, w_down)


def bwd_body(need_dx, g_ref, x_ref, a_ref, wu_ref, wd_ref, dw_ref, *rest):
    if need_dx:
        go_ref, u_s, z_s, dp_s, acc_s = rest
    else:
        u_s, z_s, dp_s = rest
    c = pl.program_id(0)
    last = pl.num_programs(0) - 1
    rb = u_s.shape[0] // ROW_BLOCKS
    width = u_s.shape[1]
    ch = z_s.shape[1]

    @pl.when(c == 0)
    def _():
        @pl.loop(0, ROW_BLOCKS)
        def _(r):
            rs = row_slice(r, rb)
            u_s[rs, :] = norm_rows(x_ref[rs, :].astype(F32)).astype(BF)
            if need_dx:
                acc_s[rs, :] = jnp.zeros((rb, width), F32)

    wd = wd_ref[...].astype(BF)
    wu = wu_ref[...].astype(BF) if need_dx else None

    def grad_pre(r):
        rs = pl.ds(r * rb, rb)
        dz = lax.dot_general(g_ref[rs, :], wd, CONTRACT_LAST, preferred_element_type=F32)
        dz = dz.astype(BF).astype(F32)
        a = a_ref[rs, :].astype(F32)
        a2 = a * a
        t = jnp.tanh(a * (GELU_A + GELU_B * a2))
        s = 0.5 + 0.5 * t
        z = a * s
        slope = s + (z * (0.5 - 0.5 * t)) * (2 * GELU_A + (6 * GELU_B) * a2)
        dp = (slope * dz).astype(BF)
        z_s[rs, :] = z.astype(BF)
        dp_s[rs, :] = dp
        return dp

    dp = grad_pre(0)
    for r in range(ROW_BLOCKS):
        dp_next = grad_pre(r + 1) if r + 1 < ROW_BLOCKS else None
        if need_dx:
            du = lax.dot_general(dp, wu, CONTRACT_LAST, preferred_element_type=F32)
            acc_s[pl.ds(r * rb, rb), :] += du
        dp = dp_next

    dwd = lax.dot_general(z_s[...], g_ref[...], CONTRACT_ROWS, preferred_element_type=F32)
    dwd = dwd.astype(BF)
    dwu = lax.dot_general(u_s[...], dp_s[...], CONTRACT_ROWS, preferred_element_type=F32)
    dw_ref[0:width, :] = dwu.astype(BF)
    for part in range(width // ch):
        dw_ref[width + part * ch:width + (part + 1) * ch, :] = dwd[:, part * ch:(part + 1) * ch]

    if need_dx:
        @pl.when(c == last)
        def _():
            @pl.loop(0, ROW_BLOCKS)
            def _(r):
                rs = row_slice(r, rb)
                xw = x_ref[rs, :].astype(F32)
                centered = xw - jnp.mean(xw, axis=-1, keepdims=True)
                var_v = jnp.mean(centered * centered, axis=-1, keepdims=True)
                rstd = lax.rsqrt(var_v + LN_EPS)
                xhat = centered * rstd
                du = acc_s[rs, :].astype(BF).astype(F32)
                m1 = jnp.mean(du, axis=-1, keepdims=True)
                m2 = jnp.mean(du * xhat, axis=-1, keepdims=True)
                dx = rstd * (du - m1 - xhat * m2)
                go_ref[rs, :] = (g_ref[rs, :].astype(F32) + dx).astype(BF)


def bwd_block(g, x, x_index, a, w_up, w_down, layer, n_chunk):
    rows, width = g.shape
    hidden = w_up.shape[2]
    ch = hidden // n_chunk
    need_dx = layer > 0
    if x.ndim == 3:
        x_spec = pl.BlockSpec((None, rows, width), lambda c: (x_index, 0, 0), pipeline_mode=ONCE)
    else:
        x_spec = pl.BlockSpec((rows, width), lambda c: (0, 0), pipeline_mode=ONCE)
    dw_rows = 2 * width
    out_specs = [pl.BlockSpec((None, dw_rows, ch), lambda c: (c, 0, 0))]
    out_shape = [jax.ShapeDtypeStruct((n_chunk, dw_rows, ch), BF)]
    scratch = [pltpu.VMEM((rows, width), BF), pltpu.VMEM((rows, ch), BF), pltpu.VMEM((rows, ch), BF)]
    if need_dx:
        out_specs.append(pl.BlockSpec((rows, width), lambda c: (0, 0), pipeline_mode=ONCE))
        out_shape.append(jax.ShapeDtypeStruct((rows, width), BF))
        scratch.append(pltpu.VMEM((rows, width), F32))
    return pl.pallas_call(
        functools.partial(bwd_body, need_dx),
        grid=(n_chunk,),
        in_specs=[
            pl.BlockSpec((rows, width), lambda c: (0, 0), pipeline_mode=ONCE),
            x_spec,
            pl.BlockSpec((None, rows, ch), lambda c: (layer, 0, c)),
            pl.BlockSpec((None, width, ch), lambda c: (layer, 0, c)),
            pl.BlockSpec((None, ch, width), lambda c: (layer, c, 0)),
        ],
        out_specs=out_specs,
        out_shape=out_shape,
        scratch_shapes=scratch,
        compiler_params=pltpu.CompilerParams(
            vmem_limit_bytes=63 * 2**20, dimension_semantics=("arbitrary",)
        ),
        cost_estimate=pl.CostEstimate(
            flops=8 * rows * width * hidden,
            bytes_accessed=12 * width * hidden + 2 * rows * (3 * width + hidden),
            transcendentals=rows * hidden,
        ),
        name="bwd_block",
    )(g, x, a, w_up, w_down)


def update_body(with_weights, n_part, me_ref, lr_ref, decay_ref, gu_ref, *refs):
    refs = list(refs)
    width = gu_ref.shape[1]
    parts, refs = refs[:n_part], refs[n_part:]
    mu_ref, md_ref = refs[:2]
    refs = refs[2:]
    if with_weights:
        wu_ref, wd_ref = refs[:2]
        refs = refs[2:]
    refs = refs[2:]
    nmu_ref, nmd_ref = refs[:2]
    decay = decay_ref[0]
    mom = decay * mu_ref[...] + gu_ref[...].astype(F32)
    nmu_ref[...] = mom
    if with_weights:
        lr = lr_ref[0]
        refs[2][...] = wu_ref[...] - lr * mom
    for p, part in enumerate(parts):
        cols = slice(p * width, (p + 1) * width)
        mom = decay * md_ref[:, cols] + part[...].astype(F32)
        nmd_ref[:, cols] = mom
        if with_weights:
            refs[3][:, cols] = wd_ref[:, cols] - lr * mom


def update_shard(me, gsum, mom_up, mom_down, w_up, w_down, bufs, layer, learn_rate, mom_decay, with_weights):
    _, width, ch = mom_up.shape
    n_part = width // ch
    steps = 4
    rows_u, rows_d = width // steps, ch // steps
    smem = pl.BlockSpec(memory_space=pltpu.SMEM)
    any_spec = pl.BlockSpec(memory_space=pl.ANY)
    up_spec = pl.BlockSpec((None, rows_u, ch), lambda c, m: (layer, c, 0))
    down_spec = pl.BlockSpec((None, rows_d, width), lambda c, m: (layer, c, 0))
    in_specs = [smem, smem, pl.BlockSpec((rows_u, ch), lambda c, m: (c, 0))]
    args = [learn_rate, mom_decay, gsum]
    for p in range(n_part):
        first = (width + p * ch) // rows_d
        in_specs.append(pl.BlockSpec((rows_d, ch), lambda c, m, first=first: (first + c, 0)))
        args.append(gsum)
    in_specs += [up_spec, down_spec]
    args += [mom_up, mom_down]
    if with_weights:
        in_specs += [
            pl.BlockSpec((None, rows_u, ch), lambda c, m: (layer, c, m[0])),
            pl.BlockSpec((None, rows_d, width), lambda c, m: (layer, m[0] * steps + c, 0)),
        ]
        args += [w_up, w_down]
    in_specs += [any_spec, any_spec]
    args += list(bufs)
    out_specs = [up_spec, down_spec]
    out_shape = [jax.ShapeDtypeStruct(mom_up.shape, F32), jax.ShapeDtypeStruct(mom_down.shape, F32)]
    if with_weights:
        out_specs += [
            pl.BlockSpec((rows_u, ch), lambda c, m: (c, 0)),
            pl.BlockSpec((rows_d, width), lambda c, m: (c, 0)),
        ]
        out_shape += [jax.ShapeDtypeStruct((width, ch), F32), jax.ShapeDtypeStruct((ch, width), F32)]
    n_in = len(args) + 1
    return pl.pallas_call(
        functools.partial(update_body, with_weights, n_part),
        grid_spec=pltpu.PrefetchScalarGridSpec(
            num_scalar_prefetch=1, grid=(steps,), in_specs=in_specs, out_specs=out_specs
        ),
        out_shape=out_shape,
        input_output_aliases={n_in - 2: 0, n_in - 1: 1},
        compiler_params=pltpu.CompilerParams(
            vmem_limit_bytes=62 * 2**20, dimension_semantics=("arbitrary",)
        ),
        cost_estimate=pl.CostEstimate(
            flops=4_000_000_000, bytes_accessed=40 * width * ch, transcendentals=0
        ),
        name="update",
    )(me, *args)


def fwd_next_body(from_grad, n_chunk, order_ref, *refs):
    refs = list(refs)
    x_ref = refs.pop(0)
    if from_grad:
        lr_ref, decay_ref, wu_ref, wd_ref, m_ref = refs[:5]
        del refs[:5]
    up_parts = refs[:n_chunk]
    down_parts = refs[n_chunk:2 * n_chunk]
    del refs[:2 * n_chunk]
    del refs[:2]
    nwu_ref, nwd_ref, xo_ref, u_s, acc_s, pu_s, pd_s, sem = refs
    c = pl.program_id(0)
    last = n_chunk - 1
    rows, width = x_ref.shape
    rb = rows // ROW_BLOCKS
    ch = pu_s.shape[2]

    def start(j, slot):
        pltpu.make_async_copy(up_parts[j], pu_s.at[slot], sem.at[0, slot]).start()
        pltpu.make_async_copy(down_parts[j], pd_s.at[slot], sem.at[1, slot]).start()

    @pl.when(c == 0)
    def _():
        start(0, 0)

    for j in range(1, n_chunk):
        @pl.when(c + 1 == j)
        def _():
            start(j, j % 2)

    @pl.when(c == 0)
    def _():
        @pl.loop(0, ROW_BLOCKS)
        def _(r):
            rs = row_slice(r, rb)
            u_s[rs, :] = norm_rows(x_ref[rs, :].astype(F32)).astype(BF)
            acc_s[rs, :] = jnp.zeros((rb, width), F32)

    slot = lax.rem(c, 2)
    pltpu.make_async_copy(up_parts[0], pu_s.at[slot], sem.at[0, slot]).wait()
    pltpu.make_async_copy(down_parts[0], pd_s.at[slot], sem.at[1, slot]).wait()
    if from_grad:
        lr, decay = lr_ref[0], decay_ref[0]
        mom = decay * m_ref[0:width, :] + pu_s[slot].astype(F32)
        nwu_ref[...] = wu_ref[...] - lr * mom
        for part in range(width // ch):
            cols = slice(part * ch, (part + 1) * ch)
            m_rows = slice(width + part * ch, width + (part + 1) * ch)
            mom = decay * m_ref[m_rows, :] + pd_s[slot, :, cols].astype(F32)
            nwd_ref[:, cols] = wd_ref[:, cols] - lr * mom
    else:
        nwu_ref[...] = pu_s[slot]
        nwd_ref[...] = pd_s[slot]
    wu = nwu_ref[...].astype(BF)
    wd = nwd_ref[...].astype(BF)

    def up(r):
        a = jnp.dot(u_s[pl.ds(r * rb, rb), :], wu, preferred_element_type=F32).astype(BF)
        return gelu_tanh(a.astype(F32)).astype(BF)

    z = up(0)
    for r in range(ROW_BLOCKS):
        z_next = up(r + 1) if r + 1 < ROW_BLOCKS else None
        acc_s[pl.ds(r * rb, rb), :] += jnp.dot(z, wd, preferred_element_type=F32)
        z = z_next

    @pl.when(c == last)
    def _():
        @pl.loop(0, ROW_BLOCKS)
        def _(r):
            rs = row_slice(r, rb)
            y = acc_s[rs, :].astype(BF).astype(F32)
            xo_ref[rs, :] = (x_ref[rs, :].astype(F32) + y).astype(BF)


def fwd_next(order, x, up_parts, down_parts, bufs, layer, grad_args=None):
    rows, width = x.shape
    n_chunk = len(up_parts)
    ch = up_parts[0].shape[1]
    hidden = n_chunk * ch
    from_grad = grad_args is not None
    part_dtype = up_parts[0].dtype
    in_specs = [pl.BlockSpec((rows, width), lambda c, o: (0, 0), pipeline_mode=ONCE)]
    args = [x]
    up_spec = pl.BlockSpec((None, width, ch), lambda c, o: (layer, 0, o[c]))
    down_spec = pl.BlockSpec((None, ch, width), lambda c, o: (layer, o[c], 0))
    if from_grad:
        learn_rate, mom_decay, w_up, w_down, mom_all, mom_index = grad_args
        in_specs += [
            pl.BlockSpec(memory_space=pltpu.SMEM),
            pl.BlockSpec(memory_space=pltpu.SMEM),
            up_spec,
            down_spec,
            pl.BlockSpec((None, None, 2 * width, ch), lambda c, o: (o[c], mom_index, 0, 0)),
        ]
        args += [learn_rate, mom_decay, w_up, w_down, mom_all]
    any_spec = pl.BlockSpec(memory_space=pl.ANY)
    in_specs += [any_spec] * (2 * n_chunk + 2)
    args += list(up_parts) + list(down_parts) + list(bufs)
    n_in = len(args) + 1
    aliases = {n_in - 2: 0, n_in - 1: 1}
    return pl.pallas_call(
        functools.partial(fwd_next_body, from_grad, n_chunk),
        grid_spec=pltpu.PrefetchScalarGridSpec(
            num_scalar_prefetch=1,
            grid=(n_chunk,),
            in_specs=in_specs,
            out_specs=[
                up_spec,
                down_spec,
                pl.BlockSpec((rows, width), lambda c, o: (0, 0), pipeline_mode=ONCE),
            ],
            scratch_shapes=[
                pltpu.VMEM((rows, width), BF),
                pltpu.VMEM((rows, width), F32),
                pltpu.VMEM((2, width, ch), part_dtype),
                pltpu.VMEM((2, ch, width), part_dtype),
                pltpu.SemaphoreType.DMA((2, 2)),
            ],
        ),
        out_shape=[
            jax.ShapeDtypeStruct(bufs[0].shape, F32),
            jax.ShapeDtypeStruct(bufs[1].shape, F32),
            jax.ShapeDtypeStruct((rows, width), BF),
        ],
        input_output_aliases=aliases,
        compiler_params=pltpu.CompilerParams(
            vmem_limit_bytes=63 * 2**20, dimension_semantics=("arbitrary",)
        ),
        cost_estimate=pl.CostEstimate(
            flops=4 * rows * width * hidden,
            bytes_accessed=24 * width * hidden,
            transcendentals=rows * hidden,
        ),
        name="fwd_next",
    )(order, *args)


def alloc_body(up_ref, down_ref):
    pass


def alloc(up_shape, down_shape):
    any_spec = pl.BlockSpec(memory_space=pl.ANY)
    return pl.pallas_call(
        alloc_body,
        out_specs=[any_spec, any_spec],
        out_shape=[jax.ShapeDtypeStruct(up_shape, F32), jax.ShapeDtypeStruct(down_shape, F32)],
        compiler_params=pltpu.CompilerParams(has_side_effects=False),
        name="alloc",
    )()


def gather_pair(first, second, n_dev):
    def swap(block, bit):
        return lax.ppermute(block, "data", [(i, i ^ bit) for i in range(n_dev)])

    f2 = swap(first, 2)
    s4 = swap(second, 4)
    f4, f6 = swap(first, 4), swap(f2, 4)
    s2, s6 = swap(second, 2), swap(s4, 2)
    firsts = {0: first, 2: f2, 4: f4, 6: f6}
    seconds = {0: second, 2: s2, 4: s4, 6: s6}
    for j in (0, 2, 4, 6):
        firsts[j + 1] = swap(firsts[j], 1)
        seconds[j + 1] = swap(seconds[j], 1)
    return [firsts[j] for j in range(n_dev)], [seconds[j] for j in range(n_dev)]


def solution(mesh):
    n_dev = mesh.shape["data"]

    def local_step(x_now, x_next, labels, w_up, w_down, w_head, mom_up, mom_down, mom_head, learn_rate, mom_decay):
        n_img, n_tok, width = x_now.shape
        layers, _, hidden = w_up.shape
        ch = hidden // n_dev
        batch_total = n_img * n_dev
        n_rows = n_img * n_tok
        rows = -(-n_rows // (16 * ROW_BLOCKS)) * (16 * ROW_BLOCKS)
        me = lax.axis_index("data")
        order = jnp.bitwise_xor(me, jnp.arange(n_dev, dtype=jnp.int32)).astype(jnp.int32)

        def pad_rows(x):
            return jnp.pad(x.reshape(n_rows, width), ((0, rows - n_rows), (0, 0)))

        row_id = lax.broadcasted_iota(jnp.int32, (n_img, rows), 1)
        img_id = lax.broadcasted_iota(jnp.int32, (n_img, rows), 0)
        member = ((row_id >= img_id * n_tok) & (row_id < (img_id + 1) * n_tok)).astype(BF)

        def down_split(m):
            return jnp.concatenate([m[..., p * ch:(p + 1) * ch] for p in range(width // ch)], axis=-2)

        def down_join(m):
            return jnp.concatenate([m[p * ch:(p + 1) * ch] for p in range(width // ch)], axis=1)

        mom_pack = jnp.concatenate([mom_up[:EARLY], down_split(mom_down[:EARLY])], axis=1)
        mom_head_all = lax.all_gather(mom_head, "data", axis=0, tiled=True)
        mom_all = lax.all_gather(mom_pack, "data", axis=0)

        def head(rows_x, head_b):
            sums = jnp.dot(member, rows_x, preferred_element_type=F32)
            pooled = sums / n_tok
            normed = norm_rows(pooled).astype(BF)
            return jnp.dot(normed, head_b, preferred_element_type=F32), pooled, normed

        x0 = pad_rows(x_now)
        pre_acts, outs = fwd_now(x0, w_up, w_down, n_dev)
        head_b = w_head.astype(BF)
        logits, pooled, normed = head(outs[layers - 1], head_b)
        soft_probs = jax.nn.softmax(logits, axis=-1)
        targets = jax.nn.one_hot(labels, logits.shape[-1], dtype=F32)
        grad_logits = ((soft_probs - targets) / batch_total).astype(BF)
        grad_normed = lax.dot_general(grad_logits, head_b, CONTRACT_LAST, preferred_element_type=F32).astype(BF)
        _, norm_pull = jax.vjp(norm_rows, pooled)
        grad_pooled = norm_pull(grad_normed.astype(F32))[0]
        grad_img = (grad_pooled / n_tok).astype(BF)
        g = lax.dot_general(member, grad_img, CONTRACT_ROWS, preferred_element_type=F32).astype(BF)

        classes = logits.shape[-1]
        factors = jnp.concatenate([normed, jnp.pad(grad_logits, ((0, 0), (0, -classes % 128)))], axis=1)
        factors = lax.all_gather(factors, "data", axis=0)
        g, factors = lax.optimization_barrier((g, factors))
        head_sum = jnp.zeros(w_head.shape, F32)
        for i in range(n_dev):
            term = lax.dot_general(
                factors[i, :, :width], factors[i, :, width:width + classes], CONTRACT_ROWS,
                preferred_element_type=F32,
            )
            head_sum = head_sum + term.astype(BF).astype(F32)
        head_sum = head_sum.astype(BF).astype(F32)
        whole_mom_head = mom_decay * mom_head_all + head_sum
        head_width = mom_head.shape[0]
        new_mom_head = lax.dynamic_slice_in_dim(whole_mom_head, me * head_width, head_width, axis=0)
        new_w_head = w_head - learn_rate * whole_mom_head

        parts = [None] * layers
        mom_bufs = alloc(mom_up.shape, mom_down.shape)
        me1, lr1, decay1 = me.reshape(1), learn_rate.reshape(1), mom_decay.reshape(1)
        for layer in reversed(range(layers)):
            x_in = (outs, layer - 1) if layer > 0 else (x0, 0)
            res = bwd_block(g, x_in[0], x_in[1], pre_acts, w_up, w_down, layer, n_dev)
            dw = res[0]
            g = res[1] if layer > 0 else None
            gsum = lax.psum_scatter(dw, "data", scatter_dimension=0, tiled=True)[0]
            early = layer < EARLY
            res = update_shard(me1, gsum, mom_up, mom_down, w_up, w_down, mom_bufs, layer, lr1, decay1, not early)
            mom_bufs = res[:2]
            if early:
                cut = [gsum[:width], down_join(gsum[width:])]
            else:
                cut = res[2:]
            parts[layer] = gather_pair(cut[0], cut[1], n_dev)

        new_mom_up, new_mom_down = mom_bufs
        bufs = alloc(w_up.shape, w_down.shape)
        x = pad_rows(x_next)
        for layer in range(layers):
            grad_args = None
            if layer < EARLY:
                grad_args = (lr1, decay1, w_up, w_down, mom_all, layer)
            *bufs, x = fwd_next(order, x, parts[layer][0], parts[layer][1], bufs, layer, grad_args)
        new_w_up, new_w_down = bufs
        logits_next = head(x, new_w_head.astype(BF))[0]
        return (logits_next, new_w_up, new_w_down, new_w_head, new_mom_up, new_mom_down, new_mom_head)

    spec_up = P(None, None, "data")
    spec_down = P(None, "data", None)
    spec_head = P("data", None)

    return jax.shard_map(
        local_step,
        mesh=mesh,
        in_specs=(P("data"), P("data"), P("data"), P(), P(), P(), spec_up, spec_down, spec_head, P(), P()),
        out_specs=(P("data"), P(), P(), P(), spec_up, spec_down, spec_head),
        check_vma=False,
    )
```

time: 3260 us -> 2880 us (0.88)
  matrix products: 1560 us -> 37.1 us
  Pallas kernels: 0 us -> 1290 us
  other arithmetic: 334 us -> 11.4 us
  waiting for transfers between devices: 1100 us -> 1410 us
  local copies, waits for them, and re-layouts: 244 us -> 52.1 us
  starting transfers between devices: 0.25 us -> 44.5 us
    dot_general x50 -> x13, matrix products: 1560 us -> 36.5 us  [the longest x8 23.9 us: local_step(): lax.dot_general(factors[i, :, :width], factors[i, :, width:width + classe...]
    pallas_call x0 -> x21, Pallas kernels: none -> 1290 us  [the longest x6 615 us: bwd_block(): pl.pallas_call(functools.partial(bwd_body, need_dx), grid=(n_chunk,), in_...]
    all_gather x3 -> x2, waiting for transfers between devices: 779 us -> 71.3 us  [the longest x1 71.3 us: local_step(): mom_all = lax.all_gather(mom_pack, 'data', axis=0)]
    ppermute x0 -> x84, waiting for transfers between devices: none -> 707 us  [swap(): return lax.ppermute(block, 'data', [(i, i ^ bit) for i in range(n_dev)])]
    reduce_scatter x2 -> x6, waiting for transfers between devices: 323 us -> 625 us  [local_step(): gsum = lax.psum_scatter(dw, 'data', scatter_dimension=0, tiled=True)[0]]
    convert_element_type x11 -> x2, other arithmetic: 228 us -> 0.16 us  [the longest x1 0.09 us: local_step(): grad_logits = ((soft_probs - targets) / batch_total).astype(BF)]
    unnamed x235 -> x84, local copies, waits for them, and re-layouts: 167 us -> 15.3 us
    convert_element_type x10 -> x0, local copies, waits for them, and re-layouts: 68.7 us -> none  [the longest x4 32.5 us: block_forward(): x_wide = x_rows.astype(jnp.float32)]
  transfers between devices with their start and end apart: 6 -> 92, of which waited for: 4 -> 21; matrix products, arithmetic and copies ran while one was open for 32% -> 2% of each run, Pallas kernels for 0% -> 11%
where the time goes in v1:
time: 2880 us; the launch traced here: 2870 us
  waiting for transfers between devices  1410 us (49%)
  Pallas kernels  1290 us (45%)
  local copies, waits for them, and re-layouts  52.1 us (2%)
  starting transfers between devices  44.5 us (2%)
  matrix products  37.1 us (1%)
    ppermute x84, waiting for transfers between devices, swap(): return lax.ppermute(block, 'data', [(i, i ^ bit) for i in range(n_dev)])  707 us
    reduce_scatter x6, waiting for transfers between devices, local_step(): gsum = lax.psum_scatter(dw, 'data', scatter_dimension=0, tiled=True)[0]  625 us
    pallas_call x6, Pallas kernels, bwd_block(): pl.pallas_call(functools.partial(bwd_body, need_dx), grid=(n_chunk,), in_...  615 us
    pallas_call x6, Pallas kernels, fwd_next(): pl.pallas_call(functools.partial(fwd_next_body, from_grad, n_chunk), grid...  341 us
    pallas_call x1, Pallas kernels, fwd_now(): pl.pallas_call(fwd_now_body, grid=(layers, n_chunk), in_specs=[pl.BlockSp...  293 us
    all_gather x1, waiting for transfers between devices, local_step(): mom_all = lax.all_gather(mom_pack, 'data', axis=0)  71.3 us
  transfers between devices with their start and end apart: 92, of which 21 were waited for; matrix products, arithmetic and copies ran while one was open for 2% of the time, Pallas kernels for 11%

profile of v1, /device:TPU:0, one launch (start us, length us, event | category | flops | bytes accessed | tf_op | source)
XLA Modules:
  0.0 2871.0 jit_solution(13731629643156379297)
XLA Ops:
  24.8 293.0 %fwd_now.1 = (bf16[6,2320,4096]{2,1,0:T(8,128)(2,1)}, bf16[6,2320,1024]{2,1,0:T(8,128)(2,1)}) custom-call(bf16[2320,1024]{1,0:T(8,128)(2,1)} %pad.12.x_ref, f32[6,1024,4096]{2,1,0:T(8,128)} %refs_4_.11, f32[6,4096,1024]{2,1,0:T(8,128)} %refs_5_.5), custom_call_target="tpu_custom_call" | custom-call | flops 233538846720 | bytes 343867392 | tf_op jit(solution)/shard_map/fwd_now/pallas_call | solution.py:85
  323.4 14.9 all-gather.2
  342.1 107.2 %bwd_block.6 = (bf16[8,2048,512]{2,1,0:T(8,128)(2,1)}, bf16[2320,1024]{1,0:T(8,128)(2,1)}) custom-call(bf16[2320,1024]{1,0:T(8,128)(2,1)} %convolution_convert_fusion.g_ref, bf16[6,2320,1024]{2,1,0:T(8,128)(2,1)} %get-tuple-element.61.x_ref, bf16[6,2320,4096]{2,1,0:T(8,128)(2,1)} %get-tuple-element.63.a_ref, f32[6,1024,4096]{2,1,0:T(8,128)} %refs_4_.11, ...), custom_call_target="tpu_custom_call" | custom-call | flops 77846282240 | bytes 83591168 | tf_op jit(solution)/shard_map/bwd_block/pallas_call | solution.py:206
  449.3 107.5 %bwd_block.7 = (bf16[8,2048,512]{2,1,0:T(8,128)(2,1)}, bf16[2320,1024]{1,0:T(8,128)(2,1)}) custom-call(bf16[2320,1024]{1,0:T(8,128)(2,1)} %get-tuple-element.64.g_ref, bf16[6,2320,1024]{2,1,0:T(8,128)(2,1)} %get-tuple-element.61.x_ref, bf16[6,2320,4096]{2,1,0:T(8,128)(2,1)} %get-tuple-element.63.a_ref, f32[6,1024,4096]{2,1,0:T(8,128)} %refs_4_.11, ...), custom_call_target="tpu_custom_call" | custom-call | flops 77846282240 | bytes 83591168 | tf_op jit(solution)/shard_map/bwd_block/pallas_call | solution.py:206
  556.9 107.8 %bwd_block.8 = (bf16[8,2048,512]{2,1,0:T(8,128)(2,1)}, bf16[2320,1024]{1,0:T(8,128)(2,1)}) custom-call(bf16[2320,1024]{1,0:T(8,128)(2,1)} %get-tuple-element.65.g_ref, bf16[6,2320,1024]{2,1,0:T(8,128)(2,1)} %get-tuple-element.61.x_ref, bf16[6,2320,4096]{2,1,0:T(8,128)(2,1)} %get-tuple-element.63.a_ref, f32[6,1024,4096]{2,1,0:T(8,128)} %refs_4_.11, ...), custom_call_target="tpu_custom_call" | custom-call | flops 77846282240 | bytes 83591168 | tf_op jit(solution)/shard_map/bwd_block/pallas_call | solution.py:206
  664.6 107.5 %bwd_block.9 = (bf16[8,2048,512]{2,1,0:T(8,128)(2,1)}, bf16[2320,1024]{1,0:T(8,128)(2,1)}) custom-call(bf16[2320,1024]{1,0:T(8,128)(2,1)} %get-tuple-element.66.g_ref, bf16[6,2320,1024]{2,1,0:T(8,128)(2,1)} %get-tuple-element.61.x_ref, bf16[6,2320,4096]{2,1,0:T(8,128)(2,1)} %get-tuple-element.63.a_ref, f32[6,1024,4096]{2,1,0:T(8,128)} %refs_4_.11, ...), custom_call_target="tpu_custom_call" | custom-call | flops 77846282240 | bytes 83591168 | tf_op jit(solution)/shard_map/bwd_block/pallas_call | solution.py:206
  772.1 107.5 %bwd_block.10 = (bf16[8,2048,512]{2,1,0:T(8,128)(2,1)}, bf16[2320,1024]{1,0:T(8,128)(2,1)}) custom-call(bf16[2320,1024]{1,0:T(8,128)(2,1)} %get-tuple-element.67.g_ref, bf16[6,2320,1024]{2,1,0:T(8,128)(2,1)} %get-tuple-element.61.x_ref, bf16[6,2320,4096]{2,1,0:T(8,128)(2,1)} %get-tuple-element.63.a_ref, f32[6,1024,4096]{2,1,0:T(8,128)} %refs_4_.11, ...), custom_call_target="tpu_custom_call" | custom-call | flops 77846282240 | bytes 83591168 | tf_op jit(solution)/shard_map/bwd_block/pallas_call | solution.py:206
  879.6 77.9 %bwd_block.11 = bf16[8,2048,512]{2,1,0:T(8,128)(2,1)} custom-call(bf16[2320,1024]{1,0:T(8,128)(2,1)} %get-tuple-element.68.g_ref, bf16[2320,1024]{1,0:T(8,128)(2,1)} %pad.12.x_ref, bf16[6,2320,4096]{2,1,0:T(8,128)(2,1)} %get-tuple-element.63.a_ref, f32[6,1024,4096]{2,1,0:T(8,128)} %refs_4_.11, f32[6,4096,1024]{2,1,0:T(8,128)} %refs_5_.5), custom_call_target="tpu_custom_call" | custom-call | flops 77846282240 | bytes 83591168 | tf_op jit(solution)/shard_map/bwd_block/pallas_call | solution.py:206
  975.5 90.1 %reduce-scatter.7.cloned.1.call-done = bf16[1,2048,512]{2,1,0:T(8,128)(2,1)} async-done(((bf16[8,2048,512]{2,1,0:T(8,128)(2,1)}), bf16[1,2048,512]{2,1,0:T(8,128)(2,1)}) %reduce-scatter.7.cloned.1.call-update) | async-done | bytes 2097168 | tf_op jit(solution)/shard_map/reduce_scatter | solution.py:550
  1073.3 21.2 collective-permute-done.10.refs_18_
  1094.5 97.3 %reduce-scatter.9.cloned.1.call-done = bf16[1,2048,512]{2,1,0:T(8,128)(2,1)} async-done(((bf16[8,2048,512]{2,1,0:T(8,128)(2,1)}), bf16[1,2048,512]{2,1,0:T(8,128)(2,1)}) %reduce-scatter.9.cloned.1.call-update) | async-done | bytes 2097168 | tf_op jit(solution)/shard_map/reduce_scatter | solution.py:550
  1197.2 106.6 %reduce-scatter.17.cloned.1.call-done = bf16[1,2048,512]{2,1,0:T(8,128)(2,1)} async-done(((bf16[8,2048,512]{2,1,0:T(8,128)(2,1)}), bf16[1,2048,512]{2,1,0:T(8,128)(2,1)}) %reduce-scatter.17.cloned.1.call-update) | async-done | bytes 2097168 | tf_op jit(solution)/shard_map/reduce_scatter | solution.py:550
  1314.7 118.7 %reduce-scatter.11.cloned.1.call-done = bf16[1,2048,512]{2,1,0:T(8,128)(2,1)} async-done(((bf16[8,2048,512]{2,1,0:T(8,128)(2,1)}), bf16[1,2048,512]{2,1,0:T(8,128)(2,1)}) %reduce-scatter.11.cloned.1.call-update) | async-done | bytes 2097168 | tf_op jit(solution)/shard_map/reduce_scatter | solution.py:550
  1435.8 108.8 %reduce-scatter.15.cloned.1.call-done = bf16[1,2048,512]{2,1,0:T(8,128)(2,1)} async-done(((bf16[8,2048,512]{2,1,0:T(8,128)(2,1)}), bf16[1,2048,512]{2,1,0:T(8,128)(2,1)}) %reduce-scatter.15.cloned.1.call-update) | async-done | bytes 2097168 | tf_op jit(solution)/shard_map/reduce_scatter | solution.py:550
  1552.0 103.9 %reduce-scatter.13.cloned.1.call-done = bf16[1,2048,512]{2,1,0:T(8,128)(2,1)} async-done(((bf16[8,2048,512]{2,1,0:T(8,128)(2,1)}), bf16[1,2048,512]{2,1,0:T(8,128)(2,1)}) %reduce-scatter.13.cloned.1.call-update) | async-done | bytes 2097168 | tf_op jit(solution)/shard_map/reduce_scatter | solution.py:550
  1668.7 35.6 %collective-permute-done.38.refs_18_ = bf16[512,1024]{1,0:T(8,128)(2,1)S(1)} collective-permute-done((bf16[512,1024]{1,0:T(8,128)(2,1)}, bf16[512,1024]{1,0:T(8,128)(2,1)S(1)}, u32[]{:S(2)}, u32[]{:S(2)}) %collective-permute-start.38) | collective-permute-done | bytes 1048608 | tf_op jit(solution)/shard_map/ppermute | solution.py:462
  1706.4 108.6 %collective-permute-done.29.refs_8_ = bf16[1024,512]{1,0:T(8,128)(2,1)S(1)} collective-permute-done((bf16[1024,512]{1,0:T(8,128)(2,1)S(1)}, bf16[1024,512]{1,0:T(8,128)(2,1)S(1)}, u32[]{:S(2)}, u32[]{:S(2)}) %collective-permute-start.29) | collective-permute-done | bytes 1048608 | tf_op jit(solution)/shard_map/ppermute | solution.py:462
  1823.2 87.1 %collective-permute-done.45.refs_5_ = f32[1024,512]{1,0:T(8,128)S(1)} collective-permute-done((f32[1024,512]{1,0:T(8,128)}, f32[1024,512]{1,0:T(8,128)S(1)}, u32[]{:S(2)}, u32[]{:S(2)}) %collective-permute-start.45) | collective-permute-done | bytes 2097184 | tf_op jit(solution)/shard_map/ppermute | solution.py:462
  1911.4 43.0 %collective-permute-done.12.refs_20_ = bf16[512,1024]{1,0:T(8,128)(2,1)} collective-permute-done((bf16[512,1024]{1,0:T(8,128)(2,1)}, bf16[512,1024]{1,0:T(8,128)(2,1)}, u32[]{:S(2)}, u32[]{:S(2)}) %collective-permute-start.12) | collective-permute-done | bytes 1048608 | tf_op jit(solution)/shard_map/ppermute | solution.py:462
  1960.2 36.9 %collective-permute-done.26.refs_20_ = bf16[512,1024]{1,0:T(8,128)(2,1)} collective-permute-done((bf16[512,1024]{1,0:T(8,128)(2,1)}, bf16[512,1024]{1,0:T(8,128)(2,1)}, u32[]{:S(2)}, u32[]{:S(2)}) %collective-permute-start.26) | collective-permute-done | bytes 1048608 | tf_op jit(solution)/shard_map/ppermute | solution.py:462
  2004.2 41.4 %collective-permute-done.40.refs_20_ = bf16[512,1024]{1,0:T(8,128)(2,1)S(1)} collective-permute-done((bf16[512,1024]{1,0:T(8,128)(2,1)S(1)}, bf16[512,1024]{1,0:T(8,128)(2,1)S(1)}, u32[]{:S(2)}, u32[]{:S(2)}) %collective-permute-start.40) | collective-permute-done | bytes 1048608 | tf_op jit(solution)/shard_map/ppermute | solution.py:462
  2047.6 94.4 %collective-permute-done.33.refs_12_ = bf16[1024,512]{1,0:T(8,128)(2,1)S(1)} collective-permute-done((bf16[1024,512]{1,0:T(8,128)(2,1)S(1)}, bf16[1024,512]{1,0:T(8,128)(2,1)S(1)}, u32[]{:S(2)}, u32[]{:S(2)}) %collective-permute-start.33) | collective-permute-done | bytes 1048608 | tf_op jit(solution)/shard_map/ppermute | solution.py:462
  2153.1 82.2 %collective-permute-done.59.refs_5_ = f32[1024,512]{1,0:T(8,128)S(1)} collective-permute-done((f32[1024,512]{1,0:T(8,128)}, f32[1024,512]{1,0:T(8,128)S(1)}, u32[]{:S(2)}, u32[]{:S(2)}) %collective-permute-start.59) | collective-permute-done | bytes 2097184 | tf_op jit(solution)/shard_map/ppermute | solution.py:462
  2239.3 87.0 %collective-permute-done.71.refs_3_ = f32[1024,512]{1,0:T(8,128)} collective-permute-done((f32[1024,512]{1,0:T(8,128)}, f32[1024,512]{1,0:T(8,128)}, u32[]{:S(2)}, u32[]{:S(2)}) %collective-permute-start.71) | collective-permute-done | bytes 2097184 | tf_op jit(solution)/shard_map/ppermute | solution.py:462
  2361.4 58.3 %collective-permute-done.80.refs_13_ = f32[512,1024]{1,0:T(8,128)} collective-permute-done((f32[512,1024]{1,0:T(8,128)}, f32[512,1024]{1,0:T(8,128)}, u32[]{:S(2)}, u32[]{:S(2)}) %collective-permute-start.80) | collective-permute-done | bytes 2097184 | tf_op jit(solution)/shard_map/ppermute | solution.py:462
  2438.2 71.3 %all-gather.8.cloned.1.call-done = f32[24,2048,512]{2,1,0:T(8,128)} async-done(((f32[3,2048,512]{2,1,0:T(8,128)}), f32[24,2048,512]{2,1,0:T(8,128)}) %all-gather.8.cloned.1.call-update) | async-done | bytes 100663312 | tf_op jit(solution)/shard_map/all_gather | solution.py:504
  2509.5 58.9 %fwd_next.6 = (f32[6,1024,4096]{2,1,0:T(8,128)}, f32[6,4096,1024]{2,1,0:T(8,128)}, bf16[2320,1024]{1,0:T(8,128)(2,1)}) custom-call(s32[8]{0:T(128)} %iota_xor_fusion.order_ref, bf16[2320,1024]{1,0:T(8,128)(2,1)} %pad.11.refs_0_, f32[1]{0:T(128)} %bitcast.92.refs_1_, f32[1]{0:T(128)} %bitcast.101.refs_2_, ...), custom_call_target="tpu_custom_call", output_to_operand_aliasing={{0}: (23, {}), {1}: (24, {})} | custom-call | flops 38923141120 | bytes 100663296 | tf_op jit(solution)/shard_map/fwd_next/pallas_call | solution.py:408
  2572.0 58.9 %fwd_next.7 = (f32[6,1024,4096]{2,1,0:T(8,128)}, f32[6,4096,1024]{2,1,0:T(8,128)}, bf16[2320,1024]{1,0:T(8,128)(2,1)}) custom-call(s32[8]{0:T(128)} %iota_xor_fusion.order_ref, bf16[2320,1024]{1,0:T(8,128)(2,1)} %get-tuple-element.71.refs_0_, f32[1]{0:T(128)} %bitcast.93.refs_1_, ...), custom_call_target="tpu_custom_call", output_to_operand_aliasing={{0}: (23, {}), {1}: (24, {})} | custom-call | flops 38923141120 | bytes 100663296 | tf_op jit(solution)/shard_map/fwd_next/pallas_call | solution.py:408
  2632.0 59.1 %fwd_next.8 = (f32[6,1024,4096]{2,1,0:T(8,128)}, f32[6,4096,1024]{2,1,0:T(8,128)}, bf16[2320,1024]{1,0:T(8,128)(2,1)}) custom-call(s32[8]{0:T(128)} %iota_xor_fusion.order_ref, bf16[2320,1024]{1,0:T(8,128)(2,1)} %get-tuple-element.75.refs_0_, f32[1]{0:T(128)} %bitcast.94.refs_1_, ...), custom_call_target="tpu_custom_call", output_to_operand_aliasing={{0}: (23, {}), {1}: (24, {})} | custom-call | flops 38923141120 | bytes 100663296 | tf_op jit(solution)/shard_map/fwd_next/pallas_call | solution.py:408
  2693.5 54.6 %fwd_next.9 = (f32[6,1024,4096]{2,1,0:T(8,128)}, f32[6,4096,1024]{2,1,0:T(8,128)}, bf16[2320,1024]{1,0:T(8,128)(2,1)}) custom-call(s32[8]{0:T(128)} %iota_xor_fusion.order_ref, bf16[2320,1024]{1,0:T(8,128)(2,1)} %get-tuple-element.79.refs_0_, f32[1024,512]{1,0:T(8,128)} %get-tuple-element.89.refs_1_, ...), custom_call_target="tpu_custom_call", output_to_operand_aliasing={{0}: (18, {}), {1}: (19, {})} | custom-call | flops 38923141120 | bytes 100663296 | tf_op jit(solution)/shard_map/fwd_next/pallas_call | solution.py:408
  2749.5 54.8 %fwd_next.10 = (f32[6,1024,4096]{2,1,0:T(8,128)}, f32[6,4096,1024]{2,1,0:T(8,128)}, bf16[2320,1024]{1,0:T(8,128)(2,1)}) custom-call(s32[8]{0:T(128)} %iota_xor_fusion.order_ref, bf16[2320,1024]{1,0:T(8,128)(2,1)} %get-tuple-element.93.refs_0_, f32[1024,512]{1,0:T(8,128)} %get-tuple-element.94.refs_1_, ...), custom_call_target="tpu_custom_call", output_to_operand_aliasing={{0}: (18, {}), {1}: (19, {})} | custom-call | flops 38923141120 | bytes 100663296 | tf_op jit(solution)/shard_map/fwd_next/pallas_call | solution.py:408
  2804.4 54.6 %fwd_next.11 = (f32[6,1024,4096]{2,1,0:T(8,128)}, f32[6,4096,1024]{2,1,0:T(8,128)}, bf16[2320,1024]{1,0:T(8,128)(2,1)}) custom-call(s32[8]{0:T(128)} %iota_xor_fusion.order_ref, bf16[2320,1024]{1,0:T(8,128)(2,1)} %get-tuple-element.98.refs_0_, f32[1024,512]{1,0:T(8,128)} %get-tuple-element.99.refs_1_, ...), custom_call_target="tpu_custom_call", output_to_operand_aliasing={{0}: (18, {}), {1}: (19, {})} | custom-call | flops 38923141120 | bytes 100663296 | tf_op jit(solution)/shard_map/fwd_next/pallas_call | solution.py:408
  (313 shorter events, 198.3 us)
Async XLA Ops:
  7.2 1058.5 %reduce-scatter.7.cloned.1.call-start = ((), (), s32[]{:S(2)}) async-start(), calls=%async_computation.6 | async-start | bytes 18874368 | tf_op jit(solution)/shard_map/reduce_scatter | solution.py:550
  957.5 234.2 %reduce-scatter.9.cloned.1.call-start = ((), (), s32[]{:S(2)}) async-start(), calls=%async_computation.7 | async-start | bytes 18874368 | tf_op jit(solution)/shard_map/reduce_scatter | solution.py:550
  958.3 345.5 %reduce-scatter.17.cloned.1.call-start = ((), (), s32[]{:S(2)}) async-start(), calls=%async_computation.11 | async-start | bytes 18874368 | tf_op jit(solution)/shard_map/reduce_scatter | solution.py:550
  959.0 474.4 %reduce-scatter.11.cloned.1.call-start = ((), (), s32[]{:S(2)}) async-start(), calls=%async_computation.8 | async-start | bytes 18874368 | tf_op jit(solution)/shard_map/reduce_scatter | solution.py:550
  959.6 585.0 %reduce-scatter.15.cloned.1.call-start = ((), (), s32[]{:S(2)}) async-start(), calls=%async_computation.10 | async-start | bytes 18874368 | tf_op jit(solution)/shard_map/reduce_scatter | solution.py:550
  960.2 695.7 %reduce-scatter.13.cloned.1.call-start = ((), (), s32[]{:S(2)}) async-start(), calls=%async_computation.9 | async-start | bytes 18874368 | tf_op jit(solution)/shard_map/reduce_scatter | solution.py:550
  960.8 1389.0 %all-gather.6.cloned.1.call-start = ((), (), s32[]{:S(2)}) async-start(), calls=%async_computation.12 | async-start | bytes 4608000 | tf_op jit(solution)/shard_map/all_gather | solution.py:503
  961.5 1548.0 %all-gather.8.cloned.1.call-start = ((), (), s32[]{:S(2)}) async-start(), calls=%async_computation.13 | async-start | bytes 113246208 | tf_op jit(solution)/shard_map/all_gather | solution.py:504
  1070.2 240.9 %collective-permute-start.7 = (bf16[512,1024]{1,0:T(8,128)(2,1)}, bf16[512,1024]{1,0:T(8,128)(2,1)}, u32[]{:S(2)}, u32[]{:S(2)}) collective-permute-start(bf16[512,1024]{1,0:T(8,128)(2,1)} %pad_maximum_fusion.1.refs_14_), channel_id=1, source_target_pairs={{0,1},{1,0},{2,3},{3,2},{4,5},{5,4},{6,7},{7,6}} | collective-permute-start | bytes 3145736 | tf_op jit(solution)/shard_map/ppermute | solution.py:462
  1071.2 241.4 %collective-permute-start.1 = (bf16[1024,512]{1,0:T(8,128)(2,1)}, bf16[1024,512]{1,0:T(8,128)(2,1)}, u32[]{:S(2)}, u32[]{:S(2)}) collective-permute-start(bf16[1024,512]{1,0:T(8,128)(2,1)} %slice_bitcast_fusion.2.refs_6_), channel_id=1, source_target_pairs={{0,2},{1,3},{2,0},{3,1},{4,6},{5,7},{6,4},{7,5}} | collective-permute-start | bytes 3145736 | tf_op jit(solution)/shard_map/ppermute | solution.py:462
  1072.7 239.9 %collective-permute-start.3 = (bf16[1024,512]{1,0:T(8,128)(2,1)}, bf16[1024,512]{1,0:T(8,128)(2,1)}, u32[]{:S(2)}, u32[]{:S(2)}) collective-permute-start(bf16[1024,512]{1,0:T(8,128)(2,1)} %slice_bitcast_fusion.2.refs_6_), channel_id=1, source_target_pairs={{0,4},{1,5},{2,6},{3,7},{4,0},{5,1},{6,2},{7,3}} | collective-permute-start | bytes 3145736 | tf_op jit(solution)/shard_map/ppermute | solution.py:462
  1094.5 218.7 %collective-permute-start = (bf16[1024,512]{1,0:T(8,128)(2,1)}, bf16[1024,512]{1,0:T(8,128)(2,1)}, u32[]{:S(2)}, u32[]{:S(2)}) collective-permute-start(bf16[1024,512]{1,0:T(8,128)(2,1)} %slice_bitcast_fusion.2.refs_6_), channel_id=1, source_target_pairs={{0,1},{1,0},{2,3},{3,2},{4,5},{5,4},{6,7},{7,6}} | collective-permute-start | bytes 3145736 | tf_op jit(solution)/shard_map/ppermute | solution.py:462
  1193.3 241.3 %collective-permute-start.24 = (bf16[512,1024]{1,0:T(8,128)(2,1)S(1)}, bf16[512,1024]{1,0:T(8,128)(2,1)}, u32[]{:S(2)}, u32[]{:S(2)}) collective-permute-start(bf16[512,1024]{1,0:T(8,128)(2,1)S(1)} %pad_maximum_fusion.2.refs_14_), channel_id=1, source_target_pairs={{0,4},{1,5},{2,6},{3,7},{4,0},{5,1},{6,2},{7,3}} | collective-permute-start | bytes 3145736 | tf_op jit(solution)/shard_map/ppermute | solution.py:462
  1311.1 352.2 %collective-permute-start.22 = (bf16[512,1024]{1,0:T(8,128)(2,1)S(1)}, bf16[512,1024]{1,0:T(8,128)(2,1)}, u32[]{:S(2)}, u32[]{:S(2)}) collective-permute-start(bf16[512,1024]{1,0:T(8,128)(2,1)S(1)} %pad_maximum_fusion.2.refs_14_), channel_id=1, source_target_pairs={{0,2},{1,3},{2,0},{3,1},{4,6},{5,7},{6,4},{7,5}} | collective-permute-start | bytes 3145736 | tf_op jit(solution)/shard_map/ppermute | solution.py:462
  1312.6 352.1 %collective-permute-start.21 = (bf16[512,1024]{1,0:T(8,128)(2,1)S(1)}, bf16[512,1024]{1,0:T(8,128)(2,1)}, u32[]{:S(2)}, u32[]{:S(2)}) collective-permute-start(bf16[512,1024]{1,0:T(8,128)(2,1)S(1)} %pad_maximum_fusion.2.refs_14_), channel_id=1, source_target_pairs={{0,1},{1,0},{2,3},{3,2},{4,5},{5,4},{6,7},{7,6}} | collective-permute-start | bytes 3145736 | tf_op jit(solution)/shard_map/ppermute | solution.py:462
  1312.7 352.6 %collective-permute-start.15 = (bf16[1024,512]{1,0:T(8,128)(2,1)}, bf16[1024,512]{1,0:T(8,128)(2,1)}, u32[]{:S(2)}, u32[]{:S(2)}) collective-permute-start(bf16[1024,512]{1,0:T(8,128)(2,1)} %slice_bitcast_fusion.1.refs_6_), channel_id=1, source_target_pairs={{0,2},{1,3},{2,0},{3,1},{4,6},{5,7},{6,4},{7,5}} | collective-permute-start | bytes 3145736 | tf_op jit(solution)/shard_map/ppermute | solution.py:462
  1313.2 352.1 %collective-permute-start.17 = (bf16[1024,512]{1,0:T(8,128)(2,1)}, bf16[1024,512]{1,0:T(8,128)(2,1)}, u32[]{:S(2)}, u32[]{:S(2)}) collective-permute-start(bf16[1024,512]{1,0:T(8,128)(2,1)} %slice_bitcast_fusion.1.refs_6_), channel_id=1, source_target_pairs={{0,4},{1,5},{2,6},{3,7},{4,0},{5,1},{6,2},{7,3}} | collective-permute-start | bytes 3145736 | tf_op jit(solution)/shard_map/ppermute | solution.py:462
  1434.7 233.5 %collective-permute-start.14 = (bf16[1024,512]{1,0:T(8,128)(2,1)}, bf16[1024,512]{1,0:T(8,128)(2,1)}, u32[]{:S(2)}, u32[]{:S(2)}) collective-permute-start(bf16[1024,512]{1,0:T(8,128)(2,1)} %slice_bitcast_fusion.1.refs_6_), channel_id=1, source_target_pairs={{0,1},{1,0},{2,3},{3,2},{4,5},{5,4},{6,7},{7,6}} | collective-permute-start | bytes 3145736 | tf_op jit(solution)/shard_map/ppermute | solution.py:462
  1665.3 151.7 %collective-permute-start.43 = (f32[1024,512]{1,0:T(8,128)}, f32[1024,512]{1,0:T(8,128)S(1)}, u32[]{:S(2)}, u32[]{:S(2)}) collective-permute-start(f32[1024,512]{1,0:T(8,128)} %get-tuple-element.89.refs_1_), channel_id=1, source_target_pairs={{0,2},{1,3},{2,0},{3,1},{4,6},{5,7},{6,4},{7,5}} | collective-permute-start | bytes 6291464 | tf_op jit(solution)/shard_map/ppermute | solution.py:462
  1668.2 146.8 %collective-permute-start.29 = (bf16[1024,512]{1,0:T(8,128)(2,1)S(1)}, bf16[1024,512]{1,0:T(8,128)(2,1)S(1)}, u32[]{:S(2)}, u32[]{:S(2)}) collective-permute-start(bf16[1024,512]{1,0:T(8,128)(2,1)S(1)} %slice_bitcast_fusion.refs_6_), channel_id=1, source_target_pairs={{0,2},{1,3},{2,0},{3,1},{4,6},{5,7},{6,4},{7,5}} | collective-permute-start | bytes 3145736 | tf_op jit(solution)/shard_map/ppermute | solution.py:462
  1821.7 132.7 %collective-permute-start.12 = (bf16[512,1024]{1,0:T(8,128)(2,1)}, bf16[512,1024]{1,0:T(8,128)(2,1)}, u32[]{:S(2)}, u32[]{:S(2)}) collective-permute-start(bf16[512,1024]{1,0:T(8,128)(2,1)} %collective-permute-done.10.refs_18_), channel_id=1, source_target_pairs={{0,2},{1,3},{2,0},{3,1},{4,6},{5,7},{6,4},{7,5}} | collective-permute-start | bytes 3145736 | tf_op jit(solution)/shard_map/ppermute | solution.py:462
  2002.1 141.3 %collective-permute-start.57 = (f32[1024,512]{1,0:T(8,128)}, f32[1024,512]{1,0:T(8,128)S(1)}, u32[]{:S(2)}, u32[]{:S(2)}) collective-permute-start(f32[1024,512]{1,0:T(8,128)} %get-tuple-element.94.refs_1_), channel_id=1, source_target_pairs={{0,2},{1,3},{2,0},{3,1},{4,6},{5,7},{6,4},{7,5}} | collective-permute-start | bytes 6291464 | tf_op jit(solution)/shard_map/ppermute | solution.py:462
  2003.6 140.2 %collective-permute-start.66 = (f32[512,1024]{1,0:T(8,128)}, f32[512,1024]{1,0:T(8,128)S(1)}, u32[]{:S(2)}, u32[]{:S(2)}) collective-permute-start(f32[512,1024]{1,0:T(8,128)} %get-tuple-element.95.refs_9_), channel_id=1, source_target_pairs={{0,4},{1,5},{2,6},{3,7},{4,0},{5,1},{6,2},{7,3}} | collective-permute-start | bytes 6291464 | tf_op jit(solution)/shard_map/ppermute | solution.py:462
  2144.7 181.6 %collective-permute-start.71 = (f32[1024,512]{1,0:T(8,128)}, f32[1024,512]{1,0:T(8,128)}, u32[]{:S(2)}, u32[]{:S(2)}) collective-permute-start(f32[1024,512]{1,0:T(8,128)} %get-tuple-element.99.refs_1_), channel_id=1, source_target_pairs={{0,2},{1,3},{2,0},{3,1},{4,6},{5,7},{6,4},{7,5}} | collective-permute-start | bytes 6291464 | tf_op jit(solution)/shard_map/ppermute | solution.py:462
  2236.7 183.0 %collective-permute-start.73 = (f32[1024,512]{1,0:T(8,128)}, f32[1024,512]{1,0:T(8,128)}, u32[]{:S(2)}, u32[]{:S(2)}) collective-permute-start(f32[1024,512]{1,0:T(8,128)} %get-tuple-element.99.refs_1_), channel_id=1, source_target_pairs={{0,4},{1,5},{2,6},{3,7},{4,0},{5,1},{6,2},{7,3}} | collective-permute-start | bytes 6291464 | tf_op jit(solution)/shard_map/ppermute | solution.py:462
  2237.2 182.4 %collective-permute-start.80 = (f32[512,1024]{1,0:T(8,128)}, f32[512,1024]{1,0:T(8,128)}, u32[]{:S(2)}, u32[]{:S(2)}) collective-permute-start(f32[512,1024]{1,0:T(8,128)} %get-tuple-element.100.refs_9_), channel_id=1, source_target_pairs={{0,4},{1,5},{2,6},{3,7},{4,0},{5,1},{6,2},{7,3}} | collective-permute-start | bytes 6291464 | tf_op jit(solution)/shard_map/ppermute | solution.py:462
  2238.7 181.5 %collective-permute-start.78 = (f32[512,1024]{1,0:T(8,128)}, f32[512,1024]{1,0:T(8,128)}, u32[]{:S(2)}, u32[]{:S(2)}) collective-permute-start(f32[512,1024]{1,0:T(8,128)} %get-tuple-element.100.refs_9_), channel_id=1, source_target_pairs={{0,2},{1,3},{2,0},{3,1},{4,6},{5,7},{6,4},{7,5}} | collective-permute-start | bytes 6291464 | tf_op jit(solution)/shard_map/ppermute | solution.py:462
  2239.3 181.0 %collective-permute-start.70 = (f32[1024,512]{1,0:T(8,128)}, f32[1024,512]{1,0:T(8,128)}, u32[]{:S(2)}, u32[]{:S(2)}) collective-permute-start(f32[1024,512]{1,0:T(8,128)} %get-tuple-element.99.refs_1_), channel_id=1, source_target_pairs={{0,1},{1,0},{2,3},{3,2},{4,5},{5,4},{6,7},{7,6}} | collective-permute-start | bytes 6291464 | tf_op jit(solution)/shard_map/ppermute | solution.py:462
  2436.2 132.4 %collective-permute-start.47 = (f32[1024,512]{1,0:T(8,128)}, f32[1024,512]{1,0:T(8,128)}, u32[]{:S(2)}, u32[]{:S(2)}) collective-permute-start(f32[1024,512]{1,0:T(8,128)} %copy-done.6), channel_id=1, source_target_pairs={{0,4},{1,5},{2,6},{3,7},{4,0},{5,1},{6,2},{7,3}} | collective-permute-start | bytes 6291464 | tf_op jit(solution)/shard_map/ppermute | solution.py:462
  2436.8 132.3 %collective-permute-start.44 = (f32[1024,512]{1,0:T(8,128)}, f32[1024,512]{1,0:T(8,128)}, u32[]{:S(2)}, u32[]{:S(2)}) collective-permute-start(f32[1024,512]{1,0:T(8,128)} %copy-done.6), channel_id=1, source_target_pairs={{0,1},{1,0},{2,3},{3,2},{4,5},{5,4},{6,7},{7,6}} | collective-permute-start | bytes 6291464 | tf_op jit(solution)/shard_map/ppermute | solution.py:462
  2437.0 132.1 %collective-permute-start.54 = (f32[512,1024]{1,0:T(8,128)}, f32[512,1024]{1,0:T(8,128)}, u32[]{:S(2)}, u32[]{:S(2)}) collective-permute-start(f32[512,1024]{1,0:T(8,128)} %copy-done.7), channel_id=1, source_target_pairs={{0,2},{1,3},{2,0},{3,1},{4,6},{5,7},{6,4},{7,5}} | collective-permute-start | bytes 6291464 | tf_op jit(solution)/shard_map/ppermute | solution.py:462
  2437.7 131.9 %collective-permute-start.46 = (f32[1024,512]{1,0:T(8,128)}, f32[1024,512]{1,0:T(8,128)}, u32[]{:S(2)}, u32[]{:S(2)}) collective-permute-start(f32[1024,512]{1,0:T(8,128)} %copy-done.8), channel_id=1, source_target_pairs={{0,1},{1,0},{2,3},{3,2},{4,5},{5,4},{6,7},{7,6}} | collective-permute-start | bytes 6291464 | tf_op jit(solution)/shard_map/ppermute | solution.py:462
  (102 other events, 10211.0 us)
Sparse Core Ops, SparseCore 0:
  957.7 107.9 reduce-scatter.6
  1069.1 122.6 reduce-scatter.8
  1195.8 107.8 reduce-scatter.16
  1307.1 126.2 reduce-scatter.10
  1436.7 107.8 reduce-scatter.14
  1548.0 107.8 reduce-scatter.12
  1657.7 47.4 all-gather.5
  1707.0 802.4 all-gather.7

commit v2 on v1

--- a/solution.py
+++ b/solution.py
@@ -18,6 +18,7 @@
 ONCE = pl.Buffered(1)
 ROW_BLOCKS = 5
 EARLY = 3
+EARLY_SC = 3
 
 
 def norm_rows(values):
@@ -304,26 +305,41 @@
     )(me, *args)
 
 
-def fwd_next_body(from_grad, n_chunk, order_ref, *refs):
+def fwd_next_body(from_grad, mom_in_parts, n_chunk, order_ref, *refs):
     refs = list(refs)
     x_ref = refs.pop(0)
     if from_grad:
-        lr_ref, decay_ref, wu_ref, wd_ref, m_ref = refs[:5]
-        del refs[:5]
+        lr_ref, decay_ref, wu_ref, wd_ref = refs[:4]
+        del refs[:4]
+        if mom_in_parts:
+            mu_parts, md_parts = refs[:n_chunk], refs[n_chunk:2 * n_chunk]
+            del refs[:2 * n_chunk]
+        else:
+            m_ref = refs.pop(0)
     up_parts = refs[:n_chunk]
     down_parts = refs[n_chunk:2 * n_chunk]
     del refs[:2 * n_chunk]
     del refs[:2]
-    nwu_ref, nwd_ref, xo_ref, u_s, acc_s, pu_s, pd_s, sem = refs
+    nwu_ref, nwd_ref, xo_ref, u_s, acc_s, pu_s, pd_s, sem = refs[:8]
+    if mom_in_parts:
+        mu_s, md_s = refs[8:]
     c = pl.program_id(0)
     last = n_chunk - 1
     rows, width = x_ref.shape
     rb = rows // ROW_BLOCKS
     ch = pu_s.shape[2]
 
+    def copies(j, slot):
+        pairs = [(up_parts[j], pu_s), (down_parts[j], pd_s)]
+        if mom_in_parts:
+            pairs += [(mu_parts[j], mu_s), (md_parts[j], md_s)]
+        return [
+            pltpu.make_async_copy(src, dst.at[slot], sem.at[i, slot]) for i, (src, dst) in enumerate(pairs)
+        ]
+
     def start(j, slot):
-        pltpu.make_async_copy(up_parts[j], pu_s.at[slot], sem.at[0, slot]).start()
-        pltpu.make_async_copy(down_parts[j], pd_s.at[slot], sem.at[1, slot]).start()
+        for copy in copies(j, slot):
+            copy.start()
 
     @pl.when(c == 0)
     def _():
@@ -343,16 +359,18 @@
             acc_s[rs, :] = jnp.zeros((rb, width), F32)
 
     slot = lax.rem(c, 2)
-    pltpu.make_async_copy(up_parts[0], pu_s.at[slot], sem.at[0, slot]).wait()
-    pltpu.make_async_copy(down_parts[0], pd_s.at[slot], sem.at[1, slot]).wait()
+    for copy in copies(0, slot):
+        copy.wait()
     if from_grad:
         lr, decay = lr_ref[0], decay_ref[0]
-        mom = decay * m_ref[0:width, :] + pu_s[slot].astype(F32)
+        m_up = mu_s[slot] if mom_in_parts else m_ref[0:width, :]
+        mom = decay * m_up + pu_s[slot].astype(F32)
         nwu_ref[...] = wu_ref[...] - lr * mom
         for part in range(width // ch):
             cols = slice(part * ch, (part + 1) * ch)
             m_rows = slice(width + part * ch, width + (part + 1) * ch)
-            mom = decay * m_ref[m_rows, :] + pd_s[slot, :, cols].astype(F32)
+            m_down = md_s[slot, :, cols] if mom_in_parts else m_ref[m_rows, :]
+            mom = decay * m_down + pd_s[slot, :, cols].astype(F32)
             nwd_ref[:, cols] = wd_ref[:, cols] - lr * mom
     else:
         nwu_ref[...] = pu_s[slot]
@@ -385,28 +403,37 @@
     ch = up_parts[0].shape[1]
     hidden = n_chunk * ch
     from_grad = grad_args is not None
+    mom_in_parts = from_grad and isinstance(grad_args[4], tuple)
     part_dtype = up_parts[0].dtype
     in_specs = [pl.BlockSpec((rows, width), lambda c, o: (0, 0), pipeline_mode=ONCE)]
     args = [x]
     up_spec = pl.BlockSpec((None, width, ch), lambda c, o: (layer, 0, o[c]))
     down_spec = pl.BlockSpec((None, ch, width), lambda c, o: (layer, o[c], 0))
     if from_grad:
-        learn_rate, mom_decay, w_up, w_down, mom_all, mom_index = grad_args
+        learn_rate, mom_decay, w_up, w_down, moms, mom_index = grad_args
         in_specs += [
             pl.BlockSpec(memory_space=pltpu.SMEM),
             pl.BlockSpec(memory_space=pltpu.SMEM),
             up_spec,
             down_spec,
-            pl.BlockSpec((None, None, 2 * width, ch), lambda c, o: (o[c], mom_index, 0, 0)),
         ]
-        args += [learn_rate, mom_decay, w_up, w_down, mom_all]
+        args += [learn_rate, mom_decay, w_up, w_down]
     any_spec = pl.BlockSpec(memory_space=pl.ANY)
+    if mom_in_parts:
+        in_specs += [any_spec] * (2 * n_chunk)
+        args += list(moms[0]) + list(moms[1])
+    elif from_grad:
+        in_specs.append(pl.BlockSpec((None, None, 2 * width, ch), lambda c, o: (o[c], mom_index, 0, 0)))
+        args.append(moms)
     in_specs += [any_spec] * (2 * n_chunk + 2)
     args += list(up_parts) + list(down_parts) + list(bufs)
     n_in = len(args) + 1
     aliases = {n_in - 2: 0, n_in - 1: 1}
+    mom_scratch = []
+    if mom_in_parts:
+        mom_scratch = [pltpu.VMEM((2, width, ch), F32), pltpu.VMEM((2, ch, width), F32)]
     return pl.pallas_call(
-        functools.partial(fwd_next_body, from_grad, n_chunk),
+        functools.partial(fwd_next_body, from_grad, mom_in_parts, n_chunk),
         grid_spec=pltpu.PrefetchScalarGridSpec(
             num_scalar_prefetch=1,
             grid=(n_chunk,),
@@ -421,7 +448,8 @@
                 pltpu.VMEM((rows, width), F32),
                 pltpu.VMEM((2, width, ch), part_dtype),
                 pltpu.VMEM((2, ch, width), part_dtype),
-                pltpu.SemaphoreType.DMA((2, 2)),
+                pltpu.SemaphoreType.DMA((4, 2)),
+                *mom_scratch,
             ],
         ),
         out_shape=[
@@ -463,14 +491,14 @@
 
     f2 = swap(first, 2)
     s4 = swap(second, 4)
-    f4, f6 = swap(first, 4), swap(f2, 4)
-    s2, s6 = swap(second, 2), swap(s4, 2)
+    f4, s2 = swap(first, 4), swap(second, 2)
+    f6, s6 = swap(f2, 4), swap(s4, 2)
     firsts = {0: first, 2: f2, 4: f4, 6: f6}
     seconds = {0: second, 2: s2, 4: s4, 6: s6}
     for j in (0, 2, 4, 6):
         firsts[j + 1] = swap(firsts[j], 1)
         seconds[j + 1] = swap(seconds[j], 1)
-    return [firsts[j] for j in range(n_dev)], [seconds[j] for j in range(n_dev)]
+    return tuple(firsts[j] for j in range(n_dev)), tuple(seconds[j] for j in range(n_dev))
 
 
 def solution(mesh):
@@ -486,6 +514,8 @@
         me = lax.axis_index("data")
         order = jnp.bitwise_xor(me, jnp.arange(n_dev, dtype=jnp.int32)).astype(jnp.int32)
 
+        slot_of = ((order >> 1) & 1) + 2 * ((order >> 2) & 1) + 4 * (order & 1)
+
         def pad_rows(x):
             return jnp.pad(x.reshape(n_rows, width), ((0, rows - n_rows), (0, 0)))
 
@@ -499,8 +529,14 @@
         def down_join(m):
             return jnp.concatenate([m[p * ch:(p + 1) * ch] for p in range(width // ch)], axis=1)
 
-        mom_pack = jnp.concatenate([mom_up[:EARLY], down_split(mom_down[:EARLY])], axis=1)
-        mom_head_all = lax.all_gather(mom_head, "data", axis=0, tiled=True)
+        mom_pack = jnp.concatenate([mom_up[:EARLY_SC], down_split(mom_down[:EARLY_SC])], axis=1)
+
+        def gather_small(block):
+            for bit in (2, 4, 1):
+                other = lax.ppermute(block, "data", [(i, i ^ bit) for i in range(n_dev)])
+                block = jnp.concatenate([block, other], axis=0)
+            return jnp.take(block, slot_of, axis=0)
+
         mom_all = lax.all_gather(mom_pack, "data", axis=0)
 
         def head(rows_x, head_b):
@@ -524,8 +560,8 @@
 
         classes = logits.shape[-1]
         factors = jnp.concatenate([normed, jnp.pad(grad_logits, ((0, 0), (0, -classes % 128)))], axis=1)
-        factors = lax.all_gather(factors, "data", axis=0)
-        g, factors = lax.optimization_barrier((g, factors))
+        factors = gather_small(factors[None])
+        mom_head_all = gather_small(mom_head[None]).reshape(w_head.shape)
         head_sum = jnp.zeros(w_head.shape, F32)
         for i in range(n_dev):
             term = lax.dot_general(
@@ -539,6 +575,7 @@
         new_mom_head = lax.dynamic_slice_in_dim(whole_mom_head, me * head_width, head_width, axis=0)
         new_w_head = w_head - learn_rate * whole_mom_head
 
+        mom_parts = {l: gather_pair(mom_up[l], mom_down[l], n_dev) for l in range(EARLY_SC, EARLY)}
         parts = [None] * layers
         mom_bufs = alloc(mom_up.shape, mom_down.shape)
         me1, lr1, decay1 = me.reshape(1), learn_rate.reshape(1), mom_decay.reshape(1)
@@ -547,6 +584,11 @@
             res = bwd_block(g, x_in[0], x_in[1], pre_acts, w_up, w_down, layer, n_dev)
             dw = res[0]
             g = res[1] if layer > 0 else None
+            if layer == 2:
+                g, x_next = lax.optimization_barrier((g, x_next))
+                x_pad = pad_rows(x_next)
+            if layer == 1:
+                g, new_w_head, new_mom_head, x_pad = lax.optimization_barrier((g, new_w_head, new_mom_head, x_pad))
             gsum = lax.psum_scatter(dw, "data", scatter_dimension=0, tiled=True)[0]
             early = layer < EARLY
             res = update_shard(me1, gsum, mom_up, mom_down, w_up, w_down, mom_bufs, layer, lr1, decay1, not early)
@@ -559,11 +601,12 @@
 
         new_mom_up, new_mom_down = mom_bufs
         bufs = alloc(w_up.shape, w_down.shape)
-        x = pad_rows(x_next)
+        x = x_pad
         for layer in range(layers):
             grad_args = None
             if layer < EARLY:
-                grad_args = (lr1, decay1, w_up, w_down, mom_all, layer)
+                moms = mom_all if layer < EARLY_SC else mom_parts[layer]
+                grad_args = (lr1, decay1, w_up, w_down, moms, layer)
             *bufs, x = fwd_next(order, x, parts[layer][0], parts[layer][1], bufs, layer, grad_args)
         new_w_up, new_w_down = bufs
         logits_next = head(x, new_w_head.astype(BF))[0]

time: 2880 us -> 2790 us (0.969)
  waiting for transfers between devices: 1410 us -> 1320 us
    reduce_scatter x6, waiting for transfers between devices: 625 us -> 400 us  [local_step(): gsum = lax.psum_scatter(dw, 'data', scatter_dimension=0, tiled=True)[0]]
    ppermute x84, waiting for transfers between devices: 707 us -> 783 us  [swap(): return lax.ppermute(block, 'data', [(i, i ^ bit) for i in range(n_dev)])]
    all_gather x1, waiting for transfers between devices: 71.3 us -> 108 us  [local_step(): mom_all = lax.all_gather(mom_pack, 'data', axis=0)]
  transfers between devices with their start and end apart: 92 -> 97, of which waited for: 21 -> 26; matrix products, arithmetic and copies ran while one was open for 2% -> 3% of each run, Pallas kernels for 11% -> 14%
where the time goes in v2:
time: 2790 us
  waiting for transfers between devices  1320 us (47%)
  Pallas kernels  1290 us (46%)
  starting transfers between devices  58 us (2%)
  local copies, waits for them, and re-layouts  54.5 us (2%)
  matrix products  37.2 us (1%)
    ppermute x84, waiting for transfers between devices, swap(): return lax.ppermute(block, 'data', [(i, i ^ bit) for i in range(n_dev)])  783 us
    pallas_call x6, Pallas kernels, bwd_block(): pl.pallas_call(functools.partial(bwd_body, need_dx), grid=(n_chunk,), in_...  616 us
    reduce_scatter x6, waiting for transfers between devices, local_step(): gsum = lax.psum_scatter(dw, 'data', scatter_dimension=0, tiled=True)[0]  400 us
    pallas_call x6, Pallas kernels, fwd_next(): pl.pallas_call(functools.partial(fwd_next_body, from_grad, mom_in_parts,...  341 us
    pallas_call x1, Pallas kernels, fwd_now(): pl.pallas_call(fwd_now_body, grid=(layers, n_chunk), in_specs=[pl.BlockSp...  293 us
    all_gather x1, waiting for transfers between devices, local_step(): mom_all = lax.all_gather(mom_pack, 'data', axis=0)  108 us
  transfers between devices with their start and end apart: 97, of which 26 were waited for; matrix products, arithmetic and copies ran while one was open for 3% of the time, Pallas kernels for 14%

profile of v2, /device:TPU:0, one launch (start us, length us, event | category | flops | bytes accessed | tf_op | source)
XLA Modules:
  0.0 2787.5 jit_solution(16806068124616841848)
XLA Ops:
  24.8 293.1 %fwd_now.1 = (bf16[6,2320,4096]{2,1,0:T(8,128)(2,1)}, bf16[6,2320,1024]{2,1,0:T(8,128)(2,1)}) custom-call(bf16[2320,1024]{1,0:T(8,128)(2,1)} %pad.11.x_ref, f32[6,1024,4096]{2,1,0:T(8,128)} %refs_4_.11, f32[6,4096,1024]{2,1,0:T(8,128)} %refs_5_.5), custom_call_target="tpu_custom_call" | custom-call | flops 233538846720 | bytes 343867392 | tf_op jit(solution)/shard_map/fwd_now/pallas_call | solution.py:86
  327.3 107.7 %bwd_block.6 = (bf16[8,2048,512]{2,1,0:T(8,128)(2,1)}, bf16[2320,1024]{1,0:T(8,128)(2,1)}) custom-call(bf16[2320,1024]{1,0:T(8,128)(2,1)} %convolution_convert_fusion.g_ref, bf16[6,2320,1024]{2,1,0:T(8,128)(2,1)} %get-tuple-element.65.x_ref, bf16[6,2320,4096]{2,1,0:T(8,128)(2,1)} %get-tuple-element.66.a_ref, f32[6,1024,4096]{2,1,0:T(8,128)} %refs_4_.11, ...), custom_call_target="tpu_custom_call" | custom-call | flops 77846282240 | bytes 83591168 | tf_op jit(solution)/shard_map/bwd_block/pallas_call | solution.py:207
  435.0 107.7 %bwd_block.7 = (bf16[8,2048,512]{2,1,0:T(8,128)(2,1)}, bf16[2320,1024]{1,0:T(8,128)(2,1)}) custom-call(bf16[2320,1024]{1,0:T(8,128)(2,1)} %get-tuple-element.67.g_ref, bf16[6,2320,1024]{2,1,0:T(8,128)(2,1)} %get-tuple-element.65.x_ref, bf16[6,2320,4096]{2,1,0:T(8,128)(2,1)} %get-tuple-element.66.a_ref, f32[6,1024,4096]{2,1,0:T(8,128)} %refs_4_.11, ...), custom_call_target="tpu_custom_call" | custom-call | flops 77846282240 | bytes 83591168 | tf_op jit(solution)/shard_map/bwd_block/pallas_call | solution.py:207
  542.7 107.5 %bwd_block.8 = (bf16[8,2048,512]{2,1,0:T(8,128)(2,1)}, bf16[2320,1024]{1,0:T(8,128)(2,1)}) custom-call(bf16[2320,1024]{1,0:T(8,128)(2,1)} %get-tuple-element.68.g_ref, bf16[6,2320,1024]{2,1,0:T(8,128)(2,1)} %get-tuple-element.65.x_ref, bf16[6,2320,4096]{2,1,0:T(8,128)(2,1)} %get-tuple-element.66.a_ref, f32[6,1024,4096]{2,1,0:T(8,128)} %refs_4_.11, ...), custom_call_target="tpu_custom_call" | custom-call | flops 77846282240 | bytes 83591168 | tf_op jit(solution)/shard_map/bwd_block/pallas_call | solution.py:207
  650.2 107.5 %bwd_block.9 = (bf16[8,2048,512]{2,1,0:T(8,128)(2,1)}, bf16[2320,1024]{1,0:T(8,128)(2,1)}) custom-call(bf16[2320,1024]{1,0:T(8,128)(2,1)} %get-tuple-element.69.g_ref, bf16[6,2320,1024]{2,1,0:T(8,128)(2,1)} %get-tuple-element.65.x_ref, bf16[6,2320,4096]{2,1,0:T(8,128)(2,1)} %get-tuple-element.66.a_ref, f32[6,1024,4096]{2,1,0:T(8,128)} %refs_4_.11, ...), custom_call_target="tpu_custom_call" | custom-call | flops 77846282240 | bytes 83591168 | tf_op jit(solution)/shard_map/bwd_block/pallas_call | solution.py:207
  757.8 107.7 %bwd_block.10 = (bf16[8,2048,512]{2,1,0:T(8,128)(2,1)}, bf16[2320,1024]{1,0:T(8,128)(2,1)}) custom-call(bf16[2320,1024]{1,0:T(8,128)(2,1)} %get-tuple-element.71.g_ref, bf16[6,2320,1024]{2,1,0:T(8,128)(2,1)} %get-tuple-element.65.x_ref, bf16[6,2320,4096]{2,1,0:T(8,128)(2,1)} %get-tuple-element.66.a_ref, f32[6,1024,4096]{2,1,0:T(8,128)} %refs_4_.11, ...), custom_call_target="tpu_custom_call" | custom-call | flops 77846282240 | bytes 83591168 | tf_op jit(solution)/shard_map/bwd_block/pallas_call | solution.py:207
  953.5 78.3 %bwd_block.11 = bf16[8,2048,512]{2,1,0:T(8,128)(2,1)} custom-call(bf16[2320,1024]{1,0:T(8,128)(2,1)} %get-tuple-element.75.g_ref, bf16[2320,1024]{1,0:T(8,128)(2,1)} %pad.11.x_ref, bf16[6,2320,4096]{2,1,0:T(8,128)(2,1)} %get-tuple-element.66.a_ref, f32[6,1024,4096]{2,1,0:T(8,128)} %refs_4_.11, f32[6,4096,1024]{2,1,0:T(8,128)} %refs_5_.5), custom_call_target="tpu_custom_call" | custom-call | flops 77846282240 | bytes 83591168 | tf_op jit(solution)/shard_map/bwd_block/pallas_call | solution.py:207
  1050.7 83.9 %reduce-scatter.11.cloned.1.call-done = bf16[1,2048,512]{2,1,0:T(8,128)(2,1)} async-done(((bf16[8,2048,512]{2,1,0:T(8,128)(2,1)}), bf16[1,2048,512]{2,1,0:T(8,128)(2,1)}) %reduce-scatter.11.cloned.1.call-update) | async-done | bytes 2097168 | tf_op jit(solution)/shard_map/reduce_scatter | solution.py:592
  1138.5 108.1 %reduce-scatter.17.cloned.1.call-done = bf16[1,2048,512]{2,1,0:T(8,128)(2,1)} async-done(((bf16[8,2048,512]{2,1,0:T(8,128)(2,1)}), bf16[1,2048,512]{2,1,0:T(8,128)(2,1)}) %reduce-scatter.17.cloned.1.call-update) | async-done | bytes 2097168 | tf_op jit(solution)/shard_map/reduce_scatter | solution.py:592
  1254.0 103.9 %reduce-scatter.15.cloned.1.call-done = bf16[1,2048,512]{2,1,0:T(8,128)(2,1)} async-done(((bf16[8,2048,512]{2,1,0:T(8,128)(2,1)}), bf16[1,2048,512]{2,1,0:T(8,128)(2,1)}) %reduce-scatter.15.cloned.1.call-update) | async-done | bytes 2097168 | tf_op jit(solution)/shard_map/reduce_scatter | solution.py:592
  1365.2 103.8 %reduce-scatter.13.cloned.1.call-done = bf16[1,2048,512]{2,1,0:T(8,128)(2,1)} async-done(((bf16[8,2048,512]{2,1,0:T(8,128)(2,1)}), bf16[1,2048,512]{2,1,0:T(8,128)(2,1)}) %reduce-scatter.13.cloned.1.call-update) | async-done | bytes 2097168 | tf_op jit(solution)/shard_map/reduce_scatter | solution.py:592
  1482.1 20.7 collective-permute-done.42.refs_16_
  1504.4 123.1 %collective-permute-done.35.refs_8_ = bf16[1024,512]{1,0:T(8,128)(2,1)S(1)} collective-permute-done((bf16[1024,512]{1,0:T(8,128)(2,1)S(1)}, bf16[1024,512]{1,0:T(8,128)(2,1)S(1)}, u32[]{:S(2)}, u32[]{:S(2)}) %collective-permute-start.35) | collective-permute-done | bytes 1048608 | tf_op jit(solution)/shard_map/ppermute | solution.py:490
  1630.9 50.1 %collective-permute-done.51.refs_5_ = f32[1024,512]{1,0:T(8,128)} collective-permute-done((f32[1024,512]{1,0:T(8,128)}, f32[1024,512]{1,0:T(8,128)}, u32[]{:S(2)}, u32[]{:S(2)}) %collective-permute-start.51) | collective-permute-done | bytes 2097184 | tf_op jit(solution)/shard_map/ppermute | solution.py:490
  1681.0 16.3 collective-permute-done.56.refs_11_
  1699.1 41.5 %collective-permute-done.32.refs_20_ = bf16[512,1024]{1,0:T(8,128)(2,1)} collective-permute-done((bf16[512,1024]{1,0:T(8,128)(2,1)S(1)}, bf16[512,1024]{1,0:T(8,128)(2,1)}, u32[]{:S(2)}, u32[]{:S(2)}) %collective-permute-start.32) | collective-permute-done | bytes 1048608 | tf_op jit(solution)/shard_map/ppermute | solution.py:490
  1748.7 41.1 %collective-permute-done.46.refs_20_ = bf16[512,1024]{1,0:T(8,128)(2,1)S(1)} collective-permute-done((bf16[512,1024]{1,0:T(8,128)(2,1)}, bf16[512,1024]{1,0:T(8,128)(2,1)S(1)}, u32[]{:S(2)}, u32[]{:S(2)}) %collective-permute-start.46) | collective-permute-done | bytes 1048608 | tf_op jit(solution)/shard_map/ppermute | solution.py:490
  1791.4 95.7 %collective-permute-done.39.refs_12_ = bf16[1024,512]{1,0:T(8,128)(2,1)} collective-permute-done((bf16[1024,512]{1,0:T(8,128)(2,1)S(1)}, bf16[1024,512]{1,0:T(8,128)(2,1)}, u32[]{:S(2)}, u32[]{:S(2)}) %collective-permute-start.39) | collective-permute-done | bytes 1048608 | tf_op jit(solution)/shard_map/ppermute | solution.py:490
  1889.8 69.7 %collective-permute-done.65.refs_5_ = f32[1024,512]{1,0:T(8,128)} collective-permute-done((f32[1024,512]{1,0:T(8,128)}, f32[1024,512]{1,0:T(8,128)}, u32[]{:S(2)}, u32[]{:S(2)}) %collective-permute-start.65) | collective-permute-done | bytes 2097184 | tf_op jit(solution)/shard_map/ppermute | solution.py:490
  1962.0 13.6 collective-permute-done.70.refs_11_
  1978.3 87.3 %collective-permute-done.77.refs_3_ = f32[1024,512]{1,0:T(8,128)} collective-permute-done((f32[1024,512]{1,0:T(8,128)}, f32[1024,512]{1,0:T(8,128)}, u32[]{:S(2)}, u32[]{:S(2)}) %collective-permute-start.77) | collective-permute-done | bytes 2097184 | tf_op jit(solution)/shard_map/ppermute | solution.py:490
  2066.1 77.0 %collective-permute-done.79.refs_5_ = f32[1024,512]{1,0:T(8,128)} collective-permute-done((f32[1024,512]{1,0:T(8,128)}, f32[1024,512]{1,0:T(8,128)}, u32[]{:S(2)}, u32[]{:S(2)}) %collective-permute-start.79) | collective-permute-done | bytes 2097184 | tf_op jit(solution)/shard_map/ppermute | solution.py:490
  2159.6 43.9 %collective-permute-done.16.refs_18_ = bf16[512,1024]{1,0:T(8,128)(2,1)} collective-permute-done((bf16[512,1024]{1,0:T(8,128)(2,1)S(1)}, bf16[512,1024]{1,0:T(8,128)(2,1)}, u32[]{:S(2)}, u32[]{:S(2)}) %collective-permute-start.16) | collective-permute-done | bytes 1048608 | tf_op jit(solution)/shard_map/ppermute | solution.py:490
  2206.2 43.5 %collective-permute-done.7.refs_8_ = bf16[1024,512]{1,0:T(8,128)(2,1)} collective-permute-done((bf16[1024,512]{1,0:T(8,128)(2,1)S(1)}, bf16[1024,512]{1,0:T(8,128)(2,1)}, u32[]{:S(2)}, u32[]{:S(2)}) %collective-permute-start.7) | collective-permute-done | bytes 1048608 | tf_op jit(solution)/shard_map/ppermute | solution.py:490
  2251.9 42.5 %collective-permute-done.18.refs_20_ = bf16[512,1024]{1,0:T(8,128)(2,1)} collective-permute-done((bf16[512,1024]{1,0:T(8,128)(2,1)}, bf16[512,1024]{1,0:T(8,128)(2,1)}, u32[]{:S(2)}, u32[]{:S(2)}) %collective-permute-start.18) | collective-permute-done | bytes 1048608 | tf_op jit(solution)/shard_map/ppermute | solution.py:490
  2318.0 108.4 %all-gather.3.cloned.1.call-done = f32[24,2048,512]{2,1,0:T(8,128)} async-done(((f32[3,2048,512]{2,1,0:T(8,128)}), f32[24,2048,512]{2,1,0:T(8,128)}) %all-gather.3.cloned.1.call-update) | async-done | bytes 100663312 | tf_op jit(solution)/shard_map/all_gather | solution.py:540
  2426.4 59.0 %fwd_next.6 = (f32[6,1024,4096]{2,1,0:T(8,128)}, f32[6,4096,1024]{2,1,0:T(8,128)}, bf16[2320,1024]{1,0:T(8,128)(2,1)}) custom-call(s32[8]{0:T(128)} %iota_xor_fusion.order_ref, bf16[2320,1024]{1,0:T(8,128)(2,1)} %pad.13.refs_0_, f32[1]{0:T(128)} %bitcast.106.refs_1_, f32[1]{0:T(128)} %bitcast.115.refs_2_, ...), custom_call_target="tpu_custom_call", output_to_operand_aliasing={{0}: (23, {}), {1}: (24, {})} | custom-call | flops 38923141120 | bytes 100663296 | tf_op jit(solution)/shard_map/fwd_next/pallas_call | solution.py:435
  2488.3 59.1 %fwd_next.7 = (f32[6,1024,4096]{2,1,0:T(8,128)}, f32[6,4096,1024]{2,1,0:T(8,128)}, bf16[2320,1024]{1,0:T(8,128)(2,1)}) custom-call(s32[8]{0:T(128)} %iota_xor_fusion.order_ref, bf16[2320,1024]{1,0:T(8,128)(2,1)} %get-tuple-element.78.refs_0_, f32[1]{0:T(128)} %bitcast.107.refs_1_, ...), custom_call_target="tpu_custom_call", output_to_operand_aliasing={{0}: (23, {}), {1}: (24, {})} | custom-call | flops 38923141120 | bytes 100663296 | tf_op jit(solution)/shard_map/fwd_next/pallas_call | solution.py:435
  2548.5 59.0 %fwd_next.8 = (f32[6,1024,4096]{2,1,0:T(8,128)}, f32[6,4096,1024]{2,1,0:T(8,128)}, bf16[2320,1024]{1,0:T(8,128)(2,1)}) custom-call(s32[8]{0:T(128)} %iota_xor_fusion.order_ref, bf16[2320,1024]{1,0:T(8,128)(2,1)} %get-tuple-element.82.refs_0_, f32[1]{0:T(128)} %bitcast.108.refs_1_, ...), custom_call_target="tpu_custom_call", output_to_operand_aliasing={{0}: (23, {}), {1}: (24, {})} | custom-call | flops 38923141120 | bytes 100663296 | tf_op jit(solution)/shard_map/fwd_next/pallas_call | solution.py:435
  2610.4 54.5 %fwd_next.9 = (f32[6,1024,4096]{2,1,0:T(8,128)}, f32[6,4096,1024]{2,1,0:T(8,128)}, bf16[2320,1024]{1,0:T(8,128)(2,1)}) custom-call(s32[8]{0:T(128)} %iota_xor_fusion.order_ref, bf16[2320,1024]{1,0:T(8,128)(2,1)} %get-tuple-element.86.refs_0_, f32[1024,512]{1,0:T(8,128)} %get-tuple-element.96.refs_1_, ...), custom_call_target="tpu_custom_call", output_to_operand_aliasing={{0}: (18, {}), {1}: (19, {})} | custom-call | flops 38923141120 | bytes 100663296 | tf_op jit(solution)/shard_map/fwd_next/pallas_call | solution.py:435
  2666.1 54.7 %fwd_next.10 = (f32[6,1024,4096]{2,1,0:T(8,128)}, f32[6,4096,1024]{2,1,0:T(8,128)}, bf16[2320,1024]{1,0:T(8,128)(2,1)}) custom-call(s32[8]{0:T(128)} %iota_xor_fusion.order_ref, bf16[2320,1024]{1,0:T(8,128)(2,1)} %get-tuple-element.100.refs_0_, f32[1024,512]{1,0:T(8,128)} %get-tuple-element.101.refs_1_, ...), custom_call_target="tpu_custom_call", output_to_operand_aliasing={{0}: (18, {}), {1}: (19, {})} | custom-call | flops 38923141120 | bytes 100663296 | tf_op jit(solution)/shard_map/fwd_next/pallas_call | solution.py:435
  2720.9 54.6 %fwd_next.11 = (f32[6,1024,4096]{2,1,0:T(8,128)}, f32[6,4096,1024]{2,1,0:T(8,128)}, bf16[2320,1024]{1,0:T(8,128)(2,1)}) custom-call(s32[8]{0:T(128)} %iota_xor_fusion.order_ref, bf16[2320,1024]{1,0:T(8,128)(2,1)} %get-tuple-element.105.refs_0_, f32[1024,512]{1,0:T(8,128)} %get-tuple-element.106.refs_1_, ...), custom_call_target="tpu_custom_call", output_to_operand_aliasing={{0}: (18, {}), {1}: (19, {})} | custom-call | flops 38923141120 | bytes 100663296 | tf_op jit(solution)/shard_map/fwd_next/pallas_call | solution.py:435
  (326 shorter events, 246.2 us)
Async XLA Ops:
  7.2 1035.2 %reduce-scatter.9.cloned.1.call-start = ((), (), s32[]{:S(2)}) async-start(), calls=%async_computation.7 | async-start | bytes 18874368 | tf_op jit(solution)/shard_map/reduce_scatter | solution.py:592
  865.4 269.2 %reduce-scatter.11.cloned.1.call-start = ((), (), s32[]{:S(2)}) async-start(), calls=%async_computation.8 | async-start | bytes 18874368 | tf_op jit(solution)/shard_map/reduce_scatter | solution.py:592
  866.2 380.4 %reduce-scatter.17.cloned.1.call-start = ((), (), s32[]{:S(2)}) async-start(), calls=%async_computation.11 | async-start | bytes 18874368 | tf_op jit(solution)/shard_map/reduce_scatter | solution.py:592
  866.9 490.9 %reduce-scatter.15.cloned.1.call-start = ((), (), s32[]{:S(2)}) async-start(), calls=%async_computation.10 | async-start | bytes 18874368 | tf_op jit(solution)/shard_map/reduce_scatter | solution.py:592
  867.5 601.6 %reduce-scatter.13.cloned.1.call-start = ((), (), s32[]{:S(2)}) async-start(), calls=%async_computation.9 | async-start | bytes 18874368 | tf_op jit(solution)/shard_map/reduce_scatter | solution.py:592
  868.1 1275.0 %reduce-scatter.7.cloned.1.call-start = ((), (), s32[]{:S(2)}) async-start(), calls=%async_computation.6 | async-start | bytes 18874368 | tf_op jit(solution)/shard_map/reduce_scatter | solution.py:592
  1031.8 1394.6 %all-gather.3.cloned.1.call-start = ((), (), s32[]{:S(2)}) async-start(), calls=%async_computation.12 | async-start | bytes 113246208 | tf_op jit(solution)/shard_map/all_gather | solution.py:540
  1048.6 428.0 %collective-permute-start.27 = (bf16[512,1024]{1,0:T(8,128)(2,1)}, bf16[512,1024]{1,0:T(8,128)(2,1)}, u32[]{:S(2)}, u32[]{:S(2)}) collective-permute-start(bf16[512,1024]{1,0:T(8,128)(2,1)} %pad_maximum_fusion.4.refs_14_), channel_id=1, source_target_pairs={{0,1},{1,0},{2,3},{3,2},{4,5},{5,4},{6,7},{7,6}} | collective-permute-start | bytes 3145736 | tf_op jit(solution)/shard_map/ppermute | solution.py:490
  1049.6 428.4 %collective-permute-start.21 = (bf16[1024,512]{1,0:T(8,128)(2,1)}, bf16[1024,512]{1,0:T(8,128)(2,1)}, u32[]{:S(2)}, u32[]{:S(2)}) collective-permute-start(bf16[1024,512]{1,0:T(8,128)(2,1)} %slice_bitcast_fusion.1.refs_6_), channel_id=1, source_target_pairs={{0,2},{1,3},{2,0},{3,1},{4,6},{5,7},{6,4},{7,5}} | collective-permute-start | bytes 3145736 | tf_op jit(solution)/shard_map/ppermute | solution.py:490
  1050.7 427.4 %collective-permute-start.23 = (bf16[1024,512]{1,0:T(8,128)(2,1)}, bf16[1024,512]{1,0:T(8,128)(2,1)}, u32[]{:S(2)}, u32[]{:S(2)}) collective-permute-start(bf16[1024,512]{1,0:T(8,128)(2,1)} %slice_bitcast_fusion.1.refs_6_), channel_id=1, source_target_pairs={{0,4},{1,5},{2,6},{3,7},{4,0},{5,1},{6,2},{7,3}} | collective-permute-start | bytes 3145736 | tf_op jit(solution)/shard_map/ppermute | solution.py:490
  1137.0 343.1 %collective-permute-start.20 = (bf16[1024,512]{1,0:T(8,128)(2,1)}, bf16[1024,512]{1,0:T(8,128)(2,1)}, u32[]{:S(2)}, u32[]{:S(2)}) collective-permute-start(bf16[1024,512]{1,0:T(8,128)(2,1)} %slice_bitcast_fusion.1.refs_6_), channel_id=1, source_target_pairs={{0,1},{1,0},{2,3},{3,2},{4,5},{5,4},{6,7},{7,6}} | collective-permute-start | bytes 3145736 | tf_op jit(solution)/shard_map/ppermute | solution.py:490
  1137.0 344.7 %collective-permute-start.44 = (bf16[512,1024]{1,0:T(8,128)(2,1)}, bf16[512,1024]{1,0:T(8,128)(2,1)}, u32[]{:S(2)}, u32[]{:S(2)}) collective-permute-start(bf16[512,1024]{1,0:T(8,128)(2,1)} %pad_maximum_fusion.5.refs_14_), channel_id=1, source_target_pairs={{0,4},{1,5},{2,6},{3,7},{4,0},{5,1},{6,2},{7,3}} | collective-permute-start | bytes 3145736 | tf_op jit(solution)/shard_map/ppermute | solution.py:490
  1478.1 151.9 %collective-permute-start.49 = (f32[1024,512]{1,0:T(8,128)}, f32[1024,512]{1,0:T(8,128)}, u32[]{:S(2)}, u32[]{:S(2)}) collective-permute-start(f32[1024,512]{1,0:T(8,128)} %get-tuple-element.96.refs_1_), channel_id=1, source_target_pairs={{0,2},{1,3},{2,0},{3,1},{4,6},{5,7},{6,4},{7,5}} | collective-permute-start | bytes 6291464 | tf_op jit(solution)/shard_map/ppermute | solution.py:490
  1480.1 147.3 %collective-permute-start.35 = (bf16[1024,512]{1,0:T(8,128)(2,1)S(1)}, bf16[1024,512]{1,0:T(8,128)(2,1)S(1)}, u32[]{:S(2)}, u32[]{:S(2)}) collective-permute-start(bf16[1024,512]{1,0:T(8,128)(2,1)S(1)} %slice_bitcast_fusion.refs_6_), channel_id=1, source_target_pairs={{0,2},{1,3},{2,0},{3,1},{4,6},{5,7},{6,4},{7,5}} | collective-permute-start | bytes 3145736 | tf_op jit(solution)/shard_map/ppermute | solution.py:490
  1481.7 146.7 %collective-permute-start.37 = (bf16[1024,512]{1,0:T(8,128)(2,1)S(1)}, bf16[1024,512]{1,0:T(8,128)(2,1)S(1)}, u32[]{:S(2)}, u32[]{:S(2)}) collective-permute-start(bf16[1024,512]{1,0:T(8,128)(2,1)S(1)} %slice_bitcast_fusion.refs_6_), channel_id=1, source_target_pairs={{0,4},{1,5},{2,6},{3,7},{4,0},{5,1},{6,2},{7,3}} | collective-permute-start | bytes 3145736 | tf_op jit(solution)/shard_map/ppermute | solution.py:490
  1502.8 127.1 %collective-permute-start.34 = (bf16[1024,512]{1,0:T(8,128)(2,1)S(1)}, bf16[1024,512]{1,0:T(8,128)(2,1)S(1)}, u32[]{:S(2)}, u32[]{:S(2)}) collective-permute-start(bf16[1024,512]{1,0:T(8,128)(2,1)S(1)} %slice_bitcast_fusion.refs_6_), channel_id=1, source_target_pairs={{0,1},{1,0},{2,3},{3,2},{4,5},{5,4},{6,7},{7,6}} | collective-permute-start | bytes 3145736 | tf_op jit(solution)/shard_map/ppermute | solution.py:490
  1502.9 127.6 %collective-permute-start.58 = (f32[512,1024]{1,0:T(8,128)}, f32[512,1024]{1,0:T(8,128)}, u32[]{:S(2)}, u32[]{:S(2)}) collective-permute-start(f32[512,1024]{1,0:T(8,128)} %get-tuple-element.97.refs_9_), channel_id=1, source_target_pairs={{0,4},{1,5},{2,6},{3,7},{4,0},{5,1},{6,2},{7,3}} | collective-permute-start | bytes 6291464 | tf_op jit(solution)/shard_map/ppermute | solution.py:490
  1630.5 110.1 %collective-permute-start.32 = (bf16[512,1024]{1,0:T(8,128)(2,1)S(1)}, bf16[512,1024]{1,0:T(8,128)(2,1)}, u32[]{:S(2)}, u32[]{:S(2)}) collective-permute-start(bf16[512,1024]{1,0:T(8,128)(2,1)S(1)} %copy-done.12), channel_id=1, source_target_pairs={{0,2},{1,3},{2,0},{3,1},{4,6},{5,7},{6,4},{7,5}} | collective-permute-start | bytes 3145736 | tf_op jit(solution)/shard_map/ppermute | solution.py:490
  1746.1 142.0 %collective-permute-start.63 = (f32[1024,512]{1,0:T(8,128)}, f32[1024,512]{1,0:T(8,128)}, u32[]{:S(2)}, u32[]{:S(2)}) collective-permute-start(f32[1024,512]{1,0:T(8,128)} %get-tuple-element.101.refs_1_), channel_id=1, source_target_pairs={{0,2},{1,3},{2,0},{3,1},{4,6},{5,7},{6,4},{7,5}} | collective-permute-start | bytes 6291464 | tf_op jit(solution)/shard_map/ppermute | solution.py:490
  1748.6 140.0 %collective-permute-start.72 = (f32[512,1024]{1,0:T(8,128)}, f32[512,1024]{1,0:T(8,128)}, u32[]{:S(2)}, u32[]{:S(2)}) collective-permute-start(f32[512,1024]{1,0:T(8,128)} %get-tuple-element.102.refs_9_), channel_id=1, source_target_pairs={{0,4},{1,5},{2,6},{3,7},{4,0},{5,1},{6,2},{7,3}} | collective-permute-start | bytes 6291464 | tf_op jit(solution)/shard_map/ppermute | solution.py:490
  1789.9 97.2 %collective-permute-start.39 = (bf16[1024,512]{1,0:T(8,128)(2,1)S(1)}, bf16[1024,512]{1,0:T(8,128)(2,1)}, u32[]{:S(2)}, u32[]{:S(2)}) collective-permute-start(bf16[1024,512]{1,0:T(8,128)(2,1)S(1)} %collective-permute-done.35.refs_8_), channel_id=1, source_target_pairs={{0,4},{1,5},{2,6},{3,7},{4,0},{5,1},{6,2},{7,3}} | collective-permute-start | bytes 3145736 | tf_op jit(solution)/shard_map/ppermute | solution.py:490
  1790.9 97.3 %collective-permute-start.38 = (bf16[1024,512]{1,0:T(8,128)(2,1)S(1)}, bf16[1024,512]{1,0:T(8,128)(2,1)S(1)}, u32[]{:S(2)}, u32[]{:S(2)}) collective-permute-start(bf16[1024,512]{1,0:T(8,128)(2,1)S(1)} %collective-permute-done.37.refs_10_), channel_id=1, source_target_pairs={{0,1},{1,0},{2,3},{3,2},{4,5},{5,4},{6,7},{7,6}} | collective-permute-start | bytes 3145736 | tf_op jit(solution)/shard_map/ppermute | solution.py:490
  1888.7 176.9 %collective-permute-start.77 = (f32[1024,512]{1,0:T(8,128)}, f32[1024,512]{1,0:T(8,128)}, u32[]{:S(2)}, u32[]{:S(2)}) collective-permute-start(f32[1024,512]{1,0:T(8,128)} %get-tuple-element.106.refs_1_), channel_id=1, source_target_pairs={{0,2},{1,3},{2,0},{3,1},{4,6},{5,7},{6,4},{7,5}} | collective-permute-start | bytes 6291464 | tf_op jit(solution)/shard_map/ppermute | solution.py:490
  1959.6 106.0 %collective-permute-start.86 = (f32[512,1024]{1,0:T(8,128)}, f32[512,1024]{1,0:T(8,128)}, u32[]{:S(2)}, u32[]{:S(2)}) collective-permute-start(f32[512,1024]{1,0:T(8,128)} %get-tuple-element.107.refs_9_), channel_id=1, source_target_pairs={{0,4},{1,5},{2,6},{3,7},{4,0},{5,1},{6,2},{7,3}} | collective-permute-start | bytes 6291464 | tf_op jit(solution)/shard_map/ppermute | solution.py:490
  1975.7 167.4 %collective-permute-start.79 = (f32[1024,512]{1,0:T(8,128)}, f32[1024,512]{1,0:T(8,128)}, u32[]{:S(2)}, u32[]{:S(2)}) collective-permute-start(f32[1024,512]{1,0:T(8,128)} %get-tuple-element.106.refs_1_), channel_id=1, source_target_pairs={{0,4},{1,5},{2,6},{3,7},{4,0},{5,1},{6,2},{7,3}} | collective-permute-start | bytes 6291464 | tf_op jit(solution)/shard_map/ppermute | solution.py:490
  1977.0 177.9 %collective-permute-start.84 = (f32[512,1024]{1,0:T(8,128)}, f32[512,1024]{1,0:T(8,128)S(1)}, u32[]{:S(2)}, u32[]{:S(2)}) collective-permute-start(f32[512,1024]{1,0:T(8,128)} %get-tuple-element.107.refs_9_), channel_id=1, source_target_pairs={{0,2},{1,3},{2,0},{3,1},{4,6},{5,7},{6,4},{7,5}} | collective-permute-start | bytes 6291464 | tf_op jit(solution)/shard_map/ppermute | solution.py:490
  1978.2 176.7 %collective-permute-start.76 = (f32[1024,512]{1,0:T(8,128)}, f32[1024,512]{1,0:T(8,128)}, u32[]{:S(2)}, u32[]{:S(2)}) collective-permute-start(f32[1024,512]{1,0:T(8,128)} %get-tuple-element.106.refs_1_), channel_id=1, source_target_pairs={{0,1},{1,0},{2,3},{3,2},{4,5},{5,4},{6,7},{7,6}} | collective-permute-start | bytes 6291464 | tf_op jit(solution)/shard_map/ppermute | solution.py:490
  2314.2 171.5 %collective-permute-start.53 = (f32[1024,512]{1,0:T(8,128)}, f32[1024,512]{1,0:T(8,128)}, u32[]{:S(2)}, u32[]{:S(2)}) collective-permute-start(f32[1024,512]{1,0:T(8,128)} %collective-permute-done.49.refs_3_), channel_id=1, source_target_pairs={{0,4},{1,5},{2,6},{3,7},{4,0},{5,1},{6,2},{7,3}} | collective-permute-start | bytes 6291464 | tf_op jit(solution)/shard_map/ppermute | solution.py:490
  2315.5 171.8 %collective-permute-start.50 = (f32[1024,512]{1,0:T(8,128)}, f32[1024,512]{1,0:T(8,128)}, u32[]{:S(2)}, u32[]{:S(2)}) collective-permute-start(f32[1024,512]{1,0:T(8,128)} %collective-permute-done.49.refs_3_), channel_id=1, source_target_pairs={{0,1},{1,0},{2,3},{3,2},{4,5},{5,4},{6,7},{7,6}} | collective-permute-start | bytes 6291464 | tf_op jit(solution)/shard_map/ppermute | solution.py:490
  2315.8 171.4 %collective-permute-start.60 = (f32[512,1024]{1,0:T(8,128)}, f32[512,1024]{1,0:T(8,128)}, u32[]{:S(2)}, u32[]{:S(2)}) collective-permute-start(f32[512,1024]{1,0:T(8,128)} %collective-permute-done.58.refs_13_), channel_id=1, source_target_pairs={{0,2},{1,3},{2,0},{3,1},{4,6},{5,7},{6,4},{7,5}} | collective-permute-start | bytes 6291464 | tf_op jit(solution)/shard_map/ppermute | solution.py:490
  2317.5 170.3 %collective-permute-start.52 = (f32[1024,512]{1,0:T(8,128)}, f32[1024,512]{1,0:T(8,128)}, u32[]{:S(2)}, u32[]{:S(2)}) collective-permute-start(f32[1024,512]{1,0:T(8,128)} %collective-permute-done.51.refs_5_), channel_id=1, source_target_pairs={{0,1},{1,0},{2,3},{3,2},{4,5},{5,4},{6,7},{7,6}} | collective-permute-start | bytes 6291464 | tf_op jit(solution)/shard_map/ppermute | solution.py:490
  2317.6 167.9 %collective-permute-start.40 = (bf16[1024,512]{1,0:T(8,128)(2,1)}, bf16[1024,512]{1,0:T(8,128)(2,1)}, u32[]{:S(2)}, u32[]{:S(2)}) collective-permute-start(bf16[1024,512]{1,0:T(8,128)(2,1)} %collective-permute-done.39.refs_12_), channel_id=1, source_target_pairs={{0,1},{1,0},{2,3},{3,2},{4,5},{5,4},{6,7},{7,6}} | collective-permute-start | bytes 3145736 | tf_op jit(solution)/shard_map/ppermute | solution.py:490
  (103 other events, 8261.7 us)
Sparse Core Ops, SparseCore 0:
  865.6 118.7 reduce-scatter.8
  987.8 146.7 reduce-scatter.10
  1138.7 107.8 reduce-scatter.16
  1249.9 107.8 reduce-scatter.14
  1361.2 107.8 reduce-scatter.12
  1473.0 172.3 reduce-scatter.6
  1647.2 779.1 all-gather.2
